TPU v7x, 32 devices: a whole 2x2x4 slice. The times are simulated.
32 devices in a mesh: dp: 4 (over z), mp: 8 (over y, x, core).
Axes of the slice: x: 2, y: 2, z: 4, core: 2. Of those that a mesh axis runs over, the one named last changes fastest.
Arguments:
- tokens: bfloat16 [8, 2048, 2048], P('dp', None, 'mp'), may hold values from -6 to 6
- doc_lengths: int32 [8, 6], P('dp'), may hold values from 1 to 1024, 2048 in all within a row
- out_grad: bfloat16 [8, 2048, 2048], P('dp', None, 'mp'), may hold values from -6 to 6
- attn_gain: float32 [2048], P('mp'), may hold values from 0.25 to 1.75
- ffn_gain: float32 [2048], P('mp'), may hold values from 0.25 to 1.75
- query_base: bfloat16 [2048, 2048], P('mp'), may hold values from -0.125 to 0.125
- query_lower: float32 [2048, 16], P('mp'), may hold values from -0.125 to 0.125
- query_upper: float32 [16, 2048], replicated, may hold values from -0.3 to 0.3
- query_scale: float32 [2048], P('mp'), may hold values from 0.8 to 1.6
- key_base: bfloat16 [2048, 2048], P('mp'), may hold values from -0.125 to 0.125
- key_lower: float32 [2048, 16], P('mp'), may hold values from -0.125 to 0.125
- key_upper: float32 [16, 2048], replicated, may hold values from -0.3 to 0.3
- key_scale: float32 [2048], P('mp'), may hold values from 0.8 to 1.6
- value_base: bfloat16 [2048, 2048], P('mp'), may hold values from -0.125 to 0.125
- value_lower: float32 [2048, 16], P('mp'), may hold values from -0.125 to 0.125
- value_upper: float32 [16, 2048], replicated, may hold values from -0.3 to 0.3
- value_scale: float32 [2048], P('mp'), may hold values from 0.5 to 2
- output_base: bfloat16 [2048, 2048], P('mp'), may hold values from -0.125 to 0.125
- output_lower: float32 [2048, 16], P('mp'), may hold values from -0.125 to 0.125
- output_upper: float32 [16, 2048], replicated, may hold values from -0.3 to 0.3
- output_scale: float32 [2048], P('mp'), may hold values from 2 to 8
- gate_base: bfloat16 [2048, 5632], P('mp'), may hold values from -0.125 to 0.125
- gate_lower: float32 [2048, 16], P('mp'), may hold values from -0.125 to 0.125
- gate_upper: float32 [16, 5632], replicated, may hold values from -0.3 to 0.3
- gate_scale: float32 [5632], P('mp'), may hold values from 0.5 to 2
- lift_base: bfloat16 [2048, 5632], P('mp'), may hold values from -0.125 to 0.125
- lift_lower: float32 [2048, 16], P('mp'), may hold values from -0.125 to 0.125
- lift_upper: float32 [16, 5632], replicated, may hold values from -0.3 to 0.3
- lift_scale: float32 [5632], P('mp'), may hold values from 0.5 to 2
- down_base: bfloat16 [5632, 2048], P('mp'), may hold values from -0.078125 to 0.078125
- down_lower: float32 [5632, 16], P('mp'), may hold values from -0.078125 to 0.078125
- down_upper: float32 [16, 2048], replicated, may hold values from -0.3 to 0.3
- down_scale: float32 [2048], P('mp'), may hold values from 1 to 3
Outputs:
- out_tokens: bfloat16 [8, 2048, 2048], P('dp', None, 'mp')
- in_grad: float32 [8, 2048, 2048], P('dp', None, 'mp')
- query_lower_grad: float32 [2048, 16], P('mp')
- query_upper_grad: float32 [16, 2048], replicated
- query_scale_grad: float32 [2048], P('mp')
- key_lower_grad: float32 [2048, 16], P('mp')
- key_upper_grad: float32 [16, 2048], replicated
- key_scale_grad: float32 [2048], P('mp')
- value_lower_grad: float32 [2048, 16], P('mp')
- value_upper_grad: float32 [16, 2048], replicated
- value_scale_grad: float32 [2048], P('mp')
- output_lower_grad: float32 [2048, 16], P('mp')
- output_upper_grad: float32 [16, 2048], replicated
- output_scale_grad: float32 [2048], P('mp')
- gate_lower_grad: float32 [2048, 16], P('mp')
- gate_upper_grad: float32 [16, 5632], replicated
- gate_scale_grad: float32 [5632], P('mp')
- lift_lower_grad: float32 [2048, 16], P('mp')
- lift_upper_grad: float32 [16, 5632], replicated
- lift_scale_grad: float32 [5632], P('mp')
- down_lower_grad: float32 [5632, 16], P('mp')
- down_upper_grad: float32 [16, 2048], replicated
- down_scale_grad: float32 [2048], P('mp')
Inputs may be any that keep to these rules, and one draw needn't show every extreme that they name: `doc_lengths`: each row lists the lengths of one sequence's 5 documents in order, then the length of the padding at its end; each row sums to 2048.
All inputs are finite; a program needn't handle non-finite values.
Results may differ from a plain program's by a relative error of at most 0.035.
Values may be sent and summed in bfloat16 or wider, within the bound.
A program may use at most 320 MiB of HBM per device.

v0:
```python
import functools

import jax
import jax.numpy as jnp
from jax import lax
from jax.experimental import pallas as pl
from jax.experimental.pallas import tpu as pltpu
from jax.sharding import PartitionSpec as P


HD = 128
R = 16
RP = 128
NDOC = 5
EPSILON = 1e-05
ROPE_BASE = 10000.0
NEGATIVE = -1e30
LOG2E = 1.4426950408889634
BF = jnp.bfloat16
F32 = jnp.float32


def dot_nn(a, b):
    return lax.dot_general(a, b, (((1,), (0,)), ((), ())), preferred_element_type=F32)


def dot_nt(a, b):
    return lax.dot_general(a, b, (((1,), (1,)), ((), ())), preferred_element_type=F32)


def dot_tn(a, b):
    return lax.dot_general(a, b, (((0,), (0,)), ((), ())), preferred_element_type=F32)


def whole(shape):
    rank = len(shape)
    return pl.BlockSpec(tuple(shape), lambda i: (0,) * rank)


def rows(block, width):
    return pl.BlockSpec((block, width), lambda i: (i, 0))


def chunk_rows(count, block, width):
    return pl.BlockSpec((count, block, width), lambda i: (0, i, 0))


def sds(shape, dtype):
    return jax.ShapeDtypeStruct(tuple(shape), dtype)


def estimate(flops, bytes_accessed):
    return pl.CostEstimate(flops=int(flops), bytes_accessed=int(bytes_accessed), transcendentals=0)


def bit_of(me, k):
    return (me // (1 << k)) % 2


def chunk_of(me, half, place, levels):
    result = 0
    for k in range(levels):
        bit = bit_of(me, k)
        flip = half if k == 0 else (place >> (levels - 1 - k)) & 1
        result = result + ((1 - bit) if flip else bit) * (1 << k)
    return result


def other(me, k):
    return {"mp": me + (1 << k) * (1 - 2 * bit_of(me, k))}


def meet(me, levels):
    barrier = pltpu.get_barrier_semaphore()
    for k in range(levels):
        pl.semaphore_signal(
            barrier, inc=1, device_id=other(me, k), device_id_type=pl.DeviceIdType.MESH
        )
    pl.semaphore_wait(barrier, levels)


def scatter_scratch(count, blocks, block, width):
    levels = count.bit_length() - 1
    shapes = []
    for level in range(levels):
        size = (count >> 1, block, width) if level == 0 else (2, count >> (level + 1), block // 2, width)
        shapes += [
            pltpu.VMEM(size, BF),
            pltpu.VMEM(size, BF),
            pltpu.VMEM((blocks,) + size, BF),
            pltpu.SemaphoreType.DMA((blocks,) if level == 0 else (blocks, 2)),
            pltpu.SemaphoreType.DMA((blocks,) if level == 0 else (blocks, 2)),
        ]
    return shapes


class Scatter:
    def __init__(self, me, count, refs, out_ref):
        self.me, self.levels, self.out_ref = me, count.bit_length() - 1, out_ref
        self.count = count
        self.keep, self.send, self.land, self.sent, self.landed = (
            [refs[5 * level + n] for level in range(self.levels)] for n in range(5)
        )
        self.blocks = self.land[0].shape[0]
        self.block = self.land[0].shape[2]

    def copy(self, level, b, path):
        if level == 0:
            bit, src, at = 0, self.send[0], (b,)
        else:
            bit = level if path == 0 else self.levels - level
            src, at = self.send[level].at[path], (b, path)
        return pltpu.make_async_remote_copy(
            src_ref=src,
            dst_ref=self.land[level].at[at],
            send_sem=self.sent[level].at[at],
            recv_sem=self.landed[level].at[at],
            device_id=other(self.me, bit),
            device_id_type=pl.DeviceIdType.MESH,
        )

    def pass_on(self, level, path, places, place, value):
        upper = place >= places // 2 if path == 0 else place % 2 == 1
        at = place % (places // 2) if path == 0 else place // 2
        ref = self.send[level + 1] if upper else self.keep[level + 1]
        ref[path, at] = value.astype(BF)

    def finish(self, level, b):
        half = self.block // 2
        if level == 0:
            self.copy(0, b, 0).wait()
            places = self.count // 2
            for place in range(places):
                value = self.keep[0][place].astype(F32) + self.land[0][b, place].astype(F32)
                self.pass_on(0, 0, places, place, value[:half])
                self.pass_on(0, 1, places, place, value[half:])
        else:
            for path in range(2):
                self.copy(level, b, path).wait()
                places = self.count >> (level + 1)
                for place in range(places):
                    value = (
                        self.keep[level][path, place].astype(F32)
                        + self.land[level][b, path, place].astype(F32)
                    )
                    if level < self.levels - 1:
                        self.pass_on(level, path, places, place, value)
                    else:
                        at = pl.multiple_of(b * self.block + path * half, half)
                        self.out_ref[pl.ds(at, half), :] = value.astype(self.out_ref.dtype)
        if level < self.levels - 1:
            for path in range(2):
                self.copy(level + 1, b, path).start()

    def advance(self, step):
        for level in range(self.levels - 1, -1, -1):
            b = step - level - 1

            @pl.when((b >= 0) & (b < self.blocks))
            def _():
                self.finish(level, b)

    def chunks(self, width):
        for half in range(2):
            for place in range(self.count // 2):
                at = chunk_of(self.me, half, place, self.levels) * width
                ref = self.send[0] if half else self.keep[0]
                yield ref, place, pl.ds(pl.multiple_of(at, width), width)


def row_scratch(count, blocks, block):
    levels = count.bit_length() - 1
    return [
        pltpu.VMEM((levels, 8, block), F32),
        pltpu.VMEM((blocks, levels, 8, block), F32),
        pltpu.SemaphoreType.DMA((blocks, levels)),
        pltpu.SemaphoreType.DMA((blocks, levels)),
    ]


class RowSum:
    def __init__(self, me, refs, out_ref):
        self.me, self.out_ref = me, out_ref
        self.held, self.land, self.sent, self.landed = refs
        self.levels, _, self.block = self.held.shape
        self.blocks = self.land.shape[0]

    def copy(self, level, b):
        return pltpu.make_async_remote_copy(
            src_ref=self.held.at[level],
            dst_ref=self.land.at[b, level],
            send_sem=self.sent.at[b, level],
            recv_sem=self.landed.at[b, level],
            device_id=other(self.me, level),
            device_id_type=pl.DeviceIdType.MESH,
        )

    def begin(self, b, value):
        self.held[0] = jnp.broadcast_to(value, (self.block, 128)).T[:8]
        self.copy(0, b).start()

    def advance(self, step):
        for level in range(self.levels - 1, -1, -1):
            b = step - level - 1

            @pl.when((b >= 0) & (b < self.blocks))
            def _():
                self.copy(level, b).wait()
                value = self.held[level] + self.land[b, level]
                if level < self.levels - 1:
                    self.held[level + 1] = value
                    self.copy(level + 1, b).start()
                else:
                    at = pl.multiple_of(b * self.block, self.block)
                    column = jnp.broadcast_to(value[:1], (128, self.block)).T
                    self.out_ref[pl.ds(at, self.block), :] = column[:, :1]


def once(shape):
    rank = len(shape)
    return pl.BlockSpec(tuple(shape), lambda i: (0,) * rank, pipeline_mode=pl.Buffered(1))


def upto(last, block, width):
    return pl.BlockSpec((block, width), lambda i: (jnp.minimum(i, last), 0))


def chunk_upto(last, count, block, width):
    return pl.BlockSpec((count, block, width), lambda i: (0, jnp.minimum(i, last), 0))


def arrange_body(*refs):
    out_ref = refs[-1]
    count = out_ref.shape[0]
    at = 0
    for ref in refs[:-1]:
        size = ref.shape[1] // count
        for c in range(count):
            out_ref[c, :, at:at + size] = ref[:, c * size:(c + 1) * size]
        at += size


def arrange(values, count):
    height = values[0].shape[0]
    size = sum(v.shape[1] for v in values) // count
    block = height // 2
    return pl.pallas_call(
        arrange_body,
        grid=(2,),
        in_specs=[rows(block, v.shape[1]) for v in values],
        out_specs=chunk_rows(count, block, size),
        out_shape=sds((count, height, size), BF),
        cost_estimate=estimate(0, 4 * count * height * size),
        name="arrange",
    )(*values)


def merge_body(base_ref, l3_ref, u3_ref, l_ref, *refs):
    splits = (len(refs) - 1) // 2
    w_refs, square_ref, cross_refs = refs[:splits], refs[splits], refs[splits + 1:]

    @pl.when(pl.program_id(0) == 0)
    def _():
        for ref in (square_ref, *cross_refs):
            ref[...] = jnp.zeros_like(ref)

    value = base_ref[0].astype(F32) + dot_tn(l3_ref[...], u3_ref[...])
    low = value.astype(BF)
    at = 0
    for ref, cross_ref in zip(w_refs, cross_refs):
        ref[0] = low[:, at:at + ref.shape[2]]
        at += ref.shape[2]
        cross_ref[...] += dot_nn(l_ref[...], ref[0])
    square_ref[...] += jnp.sum(value * value, axis=0, keepdims=True)


def merge(base, lower_t, upper, splits=None):
    count, height, width = base.shape
    splits = splits or [width]
    rank = lower_t.shape[0]
    lower_high, lower_low = split_low(lower_t)
    upper_high, upper_low = split_low(2.0 * upper)
    l3 = jnp.concatenate([lower_high, lower_low, lower_high], axis=0).astype(BF)
    u3 = jnp.concatenate([upper_high, upper_high, upper_low], axis=0).astype(BF)
    return pl.pallas_call(
        merge_body,
        grid=(count,),
        in_specs=[
            pl.BlockSpec((1, height, width), lambda i: (i, 0, 0)),
            pl.BlockSpec((3 * rank, height), lambda i: (0, i)),
            whole(u3.shape),
            pl.BlockSpec((rank, height), lambda i: (0, i)),
        ],
        out_specs=[
            *[pl.BlockSpec((1, height, n), lambda i: (i, 0, 0)) for n in splits],
            whole((1, width)),
            *[whole((rank, n)) for n in splits],
        ],
        out_shape=[
            *[sds((count, height, n), BF) for n in splits],
            sds((1, width), F32),
            *[sds((rank, n), F32) for n in splits],
        ],
        cost_estimate=estimate(
            8 * count * height * width * rank, 4 * count * height * width
        ),
        name="merge",
    )(base, l3, u3, lower_t.astype(BF))


def qkv_body(tok_ref, gain_ref, w_ref, l_ref, ratio_ref, cos_ref, sin_ref,
             x_ref, y_ref, q_ref, k_ref, xl_ref, inv_ref):
    count, block, width = tok_ref.shape
    total = jnp.zeros((block, 1), F32)
    for c in range(count):
        part = tok_ref[c].astype(F32)
        total = total + jnp.sum(part * part, axis=1, keepdims=True)
    inv = lax.rsqrt(total / (count * width) + EPSILON)
    inv_ref[...] = inv
    for c in range(count):
        x_ref[:, c * width:(c + 1) * width] = (
            tok_ref[c].astype(F32) * inv * gain_ref[c]
        ).astype(BF)
    y = dot_nn(x_ref[...], w_ref[...]) * ratio_ref[...]
    xl_ref[...] = dot_nt(x_ref[...], l_ref[...]).astype(BF)
    y_ref[...] = y.astype(BF)
    cos, sin = cos_ref[...], sin_ref[...]
    for number, out_ref in ((0, q_ref), (1, k_ref)):
        for h in range(width // HD):
            v = y[:, number * width + h * HD:number * width + (h + 1) * HD]
            out_ref[:, h * HD:(h + 1) * HD] = (
                v * cos - pltpu.roll(v, HD // 2, 1) * sin
            ).astype(BF)


def qkv_forward(tok, gain, w_cat, l_cat, ratio, cos, sin, block=256):
    count, length, width = tok.shape
    depth = count * width
    return pl.pallas_call(
        qkv_body,
        grid=(length // block,),
        in_specs=[
            chunk_rows(count, block, width),
            whole(gain.shape),
            whole(w_cat.shape),
            whole(l_cat.shape),
            whole(ratio.shape),
            rows(block, HD),
            rows(block, HD),
        ],
        out_specs=[
            rows(block, depth),
            rows(block, 3 * width),
            rows(block, width),
            rows(block, width),
            rows(block, RP),
            rows(block, 1),
        ],
        out_shape=[
            sds((length, depth), BF),
            sds((length, 3 * width), BF),
            sds((length, width), BF),
            sds((length, width), BF),
            sds((length, RP), BF),
            sds((length, 1), F32),
        ],
        cost_estimate=estimate(2 * length * depth * (3 * width + RP), 6 * length * depth),
        name="qkv_forward",
    )(tok, gain, w_cat, l_cat, ratio, cos, sin)


def attend_body(lo_ref, start_ref, q_ref, k_ref, v_ref, o_ref, lse_ref, vt_ref, *, block):
    length, width = q_ref.shape
    heads = width // HD
    factor = HD ** (-0.5) * LOG2E
    for h in range(heads):
        vt_ref[h * HD:(h + 1) * HD, :] = v_ref[:, h * HD:(h + 1) * HD].T
    key_iota = lax.broadcasted_iota(jnp.int32, (block, block), 0)
    query_iota = lax.broadcasted_iota(jnp.int32, (1, block), 1)

    def query_step(i, carry):
        base = pl.multiple_of(i * block, block)
        start = start_ref[pl.ds(i, 1), :]
        place = query_iota + base
        queries = [q_ref[pl.ds(base, block), h * HD:(h + 1) * HD] for h in range(heads)]

        def key_step(j, state):
            at = pl.multiple_of(j * block, block)
            key_place = key_iota + at
            allowed = (key_place >= start) & (key_place <= place)
            result = []
            for h in range(heads):
                top, total, acc = state[h]
                keys = k_ref[pl.ds(at, block), h * HD:(h + 1) * HD]
                s = jnp.where(allowed, dot_nt(keys, queries[h]) * factor, NEGATIVE)
                new_top = jnp.maximum(top, jnp.max(s, axis=0, keepdims=True))
                scale = jnp.exp2(top - new_top)
                p = jnp.exp2(s - new_top)
                total = total * scale + jnp.sum(p, axis=0, keepdims=True)
                acc = acc * scale + dot_nn(
                    vt_ref[h * HD:(h + 1) * HD, pl.ds(at, block)], p.astype(BF)
                )
                result.append((new_top, total, acc))
            return tuple(result)

        first = tuple(
            (
                jnp.full((1, block), NEGATIVE, F32),
                jnp.zeros((1, block), F32),
                jnp.zeros((HD, block), F32),
            )
            for _ in range(heads)
        )
        state = lax.fori_loop(lo_ref[i], i + 1, key_step, first)
        for h in range(heads):
            top, total, acc = state[h]
            o_ref[pl.ds(base, block), h * HD:(h + 1) * HD] = (acc / total).T.astype(BF)
            lse_ref[h, pl.ds(i, 1), :] = top + jnp.log2(total)
        return carry

    lax.fori_loop(0, length // block, query_step, 0)


def attend_forward(lo, start, q, k, y, block):
    length, width = q.shape
    count = length // block
    return pl.pallas_call(
        functools.partial(attend_body, block=block),
        grid=(1,),
        in_specs=[
            pl.BlockSpec(memory_space=pltpu.SMEM),
            whole(start.shape),
            whole(q.shape),
            whole(k.shape),
            pl.BlockSpec((length, width), lambda i: (0, 2)),
        ],
        out_specs=[whole(q.shape), whole((width // HD, count, block))],
        out_shape=[sds(q.shape, BF), sds((width // HD, count, block), F32)],
        scratch_shapes=[pltpu.VMEM((width, length), BF)],
        cost_estimate=estimate(2 * length * length * width, 8 * length * width),
        name="attend_forward",
    )(lo, start, q, k, y)


def attend_back_body(lo_ref, start_ref, q_ref, k_ref, v_ref, do_ref, o_ref, lse_ref, cos_ref,
                     sin_ref, ratio_ref, g_ref, kt_ref, dk_ref, dv_ref, *, block):
    length, width = q_ref.shape
    heads = width // HD
    scale = HD ** (-0.5)
    factor = scale * LOG2E
    dk_ref[...] = jnp.zeros_like(dk_ref)
    dv_ref[...] = jnp.zeros_like(dv_ref)
    for h in range(heads):
        kt_ref[h * HD:(h + 1) * HD, :] = k_ref[:, h * HD:(h + 1) * HD].T
    key_iota = lax.broadcasted_iota(jnp.int32, (block, block), 0)
    query_iota = lax.broadcasted_iota(jnp.int32, (1, block), 1)

    def turn_back(grad, base):
        return (
            grad * cos_ref[pl.ds(base, block), :]
            + pltpu.roll(grad, HD // 2, 1) * sin_ref[pl.ds(base, block), :]
        )

    def query_step(i, carry):
        base = pl.multiple_of(i * block, block)
        start = start_ref[pl.ds(i, 1), :]
        place = query_iota + base
        queries, grads, deltas, lses = [], [], [], []
        for h in range(heads):
            cols = slice(h * HD, (h + 1) * HD)
            queries.append(q_ref[pl.ds(base, block), cols])
            grad = do_ref[pl.ds(base, block), cols]
            grads.append(grad)
            product = grad.astype(F32) * o_ref[pl.ds(base, block), cols].astype(F32)
            deltas.append(jnp.sum(product.T, axis=0, keepdims=True))
            lses.append(lse_ref[h, pl.ds(i, 1), :])

        def key_step(j, state):
            at = pl.multiple_of(j * block, block)
            key_place = key_iota + at
            allowed = (key_place >= start) & (key_place <= place)
            result = []
            for h in range(heads):
                cols = slice(h * HD, (h + 1) * HD)
                keys = k_ref[pl.ds(at, block), cols]
                s = dot_nt(keys, queries[h]) * factor
                p = jnp.where(allowed, jnp.exp2(s - lses[h]), 0.0)
                dp = dot_nt(v_ref[pl.ds(at, block), cols], grads[h])
                ds = (p * (dp - deltas[h])).astype(BF)
                dv_ref[pl.ds(at, block), cols] += dot_nn(p.astype(BF), grads[h])
                dk_ref[pl.ds(at, block), cols] += dot_nn(ds, queries[h])
                result.append(state[h] + dot_nn(kt_ref[cols, pl.ds(at, block)], ds))
            return tuple(result)

        first = tuple(jnp.zeros((HD, block), F32) for _ in range(heads))
        state = lax.fori_loop(lo_ref[i], i + 1, key_step, first)
        for h in range(heads):
            cols = slice(h * HD, (h + 1) * HD)
            g_ref[pl.ds(base, block), cols] = (
                turn_back(state[h].T * scale, base) * ratio_ref[:, cols]
            ).astype(BF)
        return carry

    lax.fori_loop(0, length // block, query_step, 0)

    def finish(j, carry):
        base = pl.multiple_of(j * block, block)
        for h in range(heads):
            cols = slice(h * HD, (h + 1) * HD)
            key_cols = slice(width + h * HD, width + (h + 1) * HD)
            value_cols = slice(2 * width + h * HD, 2 * width + (h + 1) * HD)
            g_ref[pl.ds(base, block), key_cols] = (
                turn_back(dk_ref[pl.ds(base, block), cols] * scale, base)
                * ratio_ref[:, key_cols]
            ).astype(BF)
            g_ref[pl.ds(base, block), value_cols] = (
                dv_ref[pl.ds(base, block), cols] * ratio_ref[:, value_cols]
            ).astype(BF)
        return carry

    lax.fori_loop(0, length // block, finish, 0)


def attend_backward(lo, start, q, k, y, grad, attended, lse, cos, sin, ratio, block):
    length, width = q.shape
    return pl.pallas_call(
        functools.partial(attend_back_body, block=block),
        grid=(1,),
        in_specs=[
            pl.BlockSpec(memory_space=pltpu.SMEM),
            whole(start.shape),
            whole(q.shape),
            whole(k.shape),
            pl.BlockSpec((length, width), lambda i: (0, 2)),
            whole(grad.shape),
            whole(attended.shape),
            whole(lse.shape),
            whole(cos.shape),
            whole(sin.shape),
            whole(ratio.shape),
        ],
        out_specs=whole((length, 3 * width)),
        out_shape=sds((length, 3 * width), BF),
        scratch_shapes=[
            pltpu.VMEM((width, length), BF),
            pltpu.VMEM((length, width), F32),
            pltpu.VMEM((length, width), F32),
        ],
        cost_estimate=estimate(5 * length * length * width, 16 * length * width),
        name="attend_backward",
    )(lo, start, q, k, y, grad, attended, lse, cos, sin, ratio)


def out_body(a_ref, w_ref, out_ref, *scratch):
    width = out_ref.shape[1]
    count = w_ref.shape[1] // width
    step, me = pl.program_id(0), lax.axis_index("mp")
    sums = Scatter(me, count, scratch, out_ref)

    @pl.when(step == 0)
    def _():
        meet(me, sums.levels)

    sums.advance(step)

    @pl.when(step < sums.blocks)
    def _():
        act = a_ref[...]
        for ref, place, cols in sums.chunks(width):
            ref[place] = dot_nn(act, w_ref[:, cols]).astype(BF)
        sums.copy(0, step, 0).start()


def out_forward(act, w, block=256):
    length, width = act.shape
    depth = w.shape[1]
    count, blocks = depth // width, length // block
    levels = count.bit_length() - 1
    return pl.pallas_call(
        out_body,
        grid=(blocks + levels,),
        in_specs=[upto(blocks - 1, block, width), once(w.shape)],
        out_specs=whole((length, width)),
        out_shape=sds((length, width), BF),
        scratch_shapes=scatter_scratch(count, blocks, block, width),
        compiler_params=pltpu.CompilerParams(collective_id=1, has_side_effects=True),
        cost_estimate=estimate(2 * length * depth * width, 40 * length * depth),
        name="out_forward",
    )(act, w)


def ffn_body(res_ref, gain_ref, gd_in_ref, gate_ref, lift_ref, down_ref,
             rg_ref, rl_ref, lgl_ref, ug_ref, ul_ref, ld_ref, ud_ref,
             down_out, back_out, inv_ref, dot_ref,
             agl_ref, bg_ref, bl_ref, ad_ref, bd_ref, sg_ref, sl_ref,
             x_ref, gd_ref, *scratch):
    count, block, width = res_ref.shape
    step, me = pl.program_id(0), lax.axis_index("mp")
    row_sums = RowSum(me, scratch[:4], dot_ref)
    half = (len(scratch) - 4) // 2
    back_sums = Scatter(me, count, scratch[4:4 + half], back_out)
    down_sums = Scatter(me, count, scratch[4 + half:], down_out)

    @pl.when(step == 0)
    def _():
        meet(me, back_sums.levels)
        for ref in (agl_ref, bg_ref, bl_ref, ad_ref, bd_ref, sg_ref, sl_ref):
            ref[...] = jnp.zeros_like(ref)

    back_sums.advance(step)
    down_sums.advance(step)
    row_sums.advance(step)

    @pl.when(step < back_sums.blocks)
    def _():
        total = jnp.zeros((block, 1), F32)
        for c in range(count):
            part = res_ref[c].astype(F32)
            total = total + jnp.sum(part * part, axis=1, keepdims=True)
        inv = lax.rsqrt(total / (count * width) + EPSILON)
        inv_ref[...] = inv
        for c in range(count):
            cols = slice(c * width, (c + 1) * width)
            x_ref[:, cols] = (res_ref[c].astype(F32) * inv * gain_ref[c]).astype(BF)
            gd_ref[:, cols] = gd_in_ref[c]
        x, grad_down = x_ref[...], gd_ref[...]
        inner_g = dot_nn(x, gate_ref[...])
        inner_u = dot_nn(x, lift_ref[...])
        gate_ratio, lift_ratio = rg_ref[...], rl_ref[...]
        gate_act, lift_act = inner_g * gate_ratio, inner_u * lift_ratio
        sigmoid_g = jax.nn.sigmoid(gate_act)
        silu_g = gate_act * sigmoid_g
        hidden = (silu_g * lift_act).astype(BF)
        for ref, place, at in down_sums.chunks(width):
            ref[place] = dot_nn(hidden, down_ref[:, at]).astype(BF)
        down_sums.copy(0, step, 0).start()
        grad_hidden = dot_nt(grad_down, down_ref[...])
        d_lift = grad_hidden * silu_g
        d_gate = grad_hidden * lift_act * sigmoid_g * (1.0 + gate_act * (1.0 - sigmoid_g))
        grad_g = (d_gate * gate_ratio).astype(BF)
        grad_l = (d_lift * lift_ratio).astype(BF)
        for ref, place, at in back_sums.chunks(width):
            ref[place] = (
                dot_nt(grad_g, gate_ref[at, :]) + dot_nt(grad_l, lift_ref[at, :])
            ).astype(BF)
        back_sums.copy(0, step, 0).start()
        product_g, product_l = inner_g * d_gate, inner_u * d_lift
        sg_ref[...] += jnp.sum(product_g, axis=0, keepdims=True)
        sl_ref[...] += jnp.sum(product_l, axis=0, keepdims=True)
        row_sums.begin(
            step,
            jnp.sum(product_g * gate_ratio + product_l * lift_ratio, axis=1, keepdims=True),
        )
        low_x = dot_nt(x, lgl_ref[...]).astype(BF)
        low_g = (dot_nt(grad_g, ug_ref[...]) + dot_nt(grad_l, ul_ref[...])).astype(BF)
        agl_ref[...] += dot_tn(low_g, x)
        bg_ref[...] += dot_tn(low_x, grad_g)
        bl_ref[...] += dot_tn(low_x, grad_l)
        low_h = dot_nn(hidden, ld_ref[...]).astype(BF)
        low_d = dot_nt(grad_down, ud_ref[...]).astype(BF)
        ad_ref[...] += dot_tn(low_d, hidden)
        bd_ref[...] += dot_tn(low_h, grad_down)


def ffn(res, gain, gd, gate, lift, down, rg, rl, lgl, ug, ul, ld, ud, block=256):
    count, length, width = res.shape
    depth, hidden = gate.shape
    blocks = length // block
    levels = count.bit_length() - 1
    acc_shapes = [
        (RP, depth), (RP, hidden), (RP, hidden), (RP, hidden), (RP, depth),
        (1, hidden), (1, hidden),
    ]
    return pl.pallas_call(
        ffn_body,
        grid=(blocks + levels,),
        in_specs=[
            chunk_upto(blocks - 1, count, block, width),
            once(gain.shape),
            chunk_upto(blocks - 1, count, block, width),
            *[once(a.shape) for a in (gate, lift, down, rg, rl, lgl, ug, ul, ld, ud)],
        ],
        out_specs=[
            whole((length, width)), whole((length, width)),
            upto(blocks - 1, block, 1), whole((length, 1)),
            *[whole(s) for s in acc_shapes],
        ],
        out_shape=[
            sds((length, width), BF), sds((length, width), BF),
            sds((length, 1), F32), sds((length, 1), F32),
            *[sds(s, F32) for s in acc_shapes],
        ],
        scratch_shapes=[
            pltpu.VMEM((block, depth), BF), pltpu.VMEM((block, depth), BF),
            *row_scratch(count, blocks, block),
            *scatter_scratch(count, blocks, block, width),
            *scatter_scratch(count, blocks, block, width),
        ],
        compiler_params=pltpu.CompilerParams(collective_id=2, has_side_effects=True),
        cost_estimate=estimate(14 * length * depth * hidden, 40 * length * depth),
        name="ffn",
    )(res, gain, gd, gate, lift, down, rg, rl, lgl, ug, ul, ld, ud)


def out_back_body(g_ref, a_ref, w_ref, u_ref, l_ref, da_ref, aa_ref, bb_ref, grad_ref):
    count, _, width = g_ref.shape

    @pl.when(pl.program_id(0) == 0)
    def _():
        aa_ref[...] = jnp.zeros_like(aa_ref)
        bb_ref[...] = jnp.zeros_like(bb_ref)

    for c in range(count):
        grad_ref[:, c * width:(c + 1) * width] = g_ref[c]
    grad, act = grad_ref[...], a_ref[...]
    da_ref[...] = dot_nt(grad, w_ref[...]).astype(BF)
    low_g = dot_nt(grad, u_ref[...]).astype(BF)
    low_a = dot_nn(act, l_ref[...]).astype(BF)
    aa_ref[...] += dot_tn(low_g, act)
    bb_ref[...] += dot_tn(low_a, grad)


def out_back(grad, act, w, u, low, block=256):
    count, length, width = grad.shape
    depth = count * width
    return pl.pallas_call(
        out_back_body,
        grid=(length // block,),
        in_specs=[
            chunk_rows(count, block, width), rows(block, width), whole(w.shape),
            whole(u.shape), whole(low.shape),
        ],
        out_specs=[rows(block, width), whole((RP, width)), whole((RP, depth))],
        out_shape=[sds((length, width), BF), sds((RP, width), F32), sds((RP, depth), F32)],
        scratch_shapes=[pltpu.VMEM((block, depth), BF)],
        cost_estimate=estimate(4 * length * depth * width, 3 * length * depth),
        name="out_back",
    )(grad, act, w, u, low)


def qkv_back_body(g_ref, y_ref, x_ref, xl_ref, w_ref, u_ref, inv_ratio_ref,
                  dx_ref, dot_ref, aa_ref, bb_ref, ss_ref, *scratch):
    width = dx_ref.shape[1]
    count = w_ref.shape[0] // width
    step, me = pl.program_id(0), lax.axis_index("mp")
    row_sums = RowSum(me, scratch[:4], dot_ref)
    sums = Scatter(me, count, scratch[4:], dx_ref)

    @pl.when(step == 0)
    def _():
        meet(me, sums.levels)
        aa_ref[...] = jnp.zeros_like(aa_ref)
        bb_ref[...] = jnp.zeros_like(bb_ref)
        ss_ref[...] = jnp.zeros_like(ss_ref)

    sums.advance(step)
    row_sums.advance(step)

    @pl.when(step < sums.blocks)
    def _():
        grad = g_ref[...]
        for ref, place, at in sums.chunks(width):
            ref[place] = dot_nt(grad, w_ref[at, :]).astype(BF)
        sums.copy(0, step, 0).start()
        product = grad.astype(F32) * y_ref[...].astype(F32) * inv_ratio_ref[...]
        row_sums.begin(step, jnp.sum(product, axis=1, keepdims=True))
        ss_ref[...] += jnp.sum(product * inv_ratio_ref[...], axis=0, keepdims=True)
        low_g = dot_nt(grad, u_ref[...]).astype(BF)
        aa_ref[...] += dot_tn(low_g, x_ref[...])
        bb_ref[...] += dot_tn(xl_ref[...], grad)


def qkv_backward(grad, y, x, xl, w_cat, u_cat, inv_ratio, count, block=256):
    length, depth = x.shape
    wide = grad.shape[1]
    width, blocks = depth // count, length // block
    levels = count.bit_length() - 1
    return pl.pallas_call(
        qkv_back_body,
        grid=(blocks + levels,),
        in_specs=[
            upto(blocks - 1, block, wide), upto(blocks - 1, block, wide),
            upto(blocks - 1, block, depth), upto(blocks - 1, block, RP),
            once(w_cat.shape), once(u_cat.shape), once(inv_ratio.shape),
        ],
        out_specs=[
            whole((length, width)), whole((length, 1)),
            whole((RP, depth)), whole((RP, wide)), whole((1, wide)),
        ],
        out_shape=[
            sds((length, width), BF), sds((length, 1), F32),
            sds((RP, depth), F32), sds((RP, wide), F32), sds((1, wide), F32),
        ],
        scratch_shapes=[
            *row_scratch(count, blocks, block), *scatter_scratch(count, blocks, block, width)
        ],
        compiler_params=pltpu.CompilerParams(collective_id=3, has_side_effects=True),
        cost_estimate=estimate(4 * length * depth * wide, 40 * length * depth),
        name="qkv_backward",
    )(grad, y, x, xl, w_cat, u_cat, inv_ratio)


def far(z, k):
    return {"dp": z + (1 << k) * (1 - 2 * bit_of(z, k))}


def reduce_body(part_ref, *refs, levels, depths, ranks, weights):
    groups, count = len(ranks), len(weights)

    def take(number):
        nonlocal refs
        taken, refs = refs[:number], refs[number:]
        return taken

    own_refs, cross_refs, coef_refs, inv_refs = (take(groups) for _ in range(4))
    base_refs, upper_refs, lower_refs = (take(count) for _ in range(3))
    scale_outs, upper_outs, lower_outs = take(groups), take(count), take(count)
    keep, send, land = (take(levels) for _ in range(3))
    sums, held, come, full, beta_refs = (take(groups) for _ in range(5))
    bases = take(count)
    sent, landed, far_sent, far_landed, full_sent, full_landed, base_sems = refs
    me, z = lax.axis_index("mp"), lax.axis_index("dp")
    loads = [
        pltpu.make_async_copy(base_refs[n], bases[n], base_sems.at[n]) for n in range(count)
    ]
    for load in loads:
        load.start()
    barrier = pltpu.get_barrier_semaphore()
    for target in [other(me, k) for k in range(levels)] + [far(z, k) for k in range(depths)]:
        pl.semaphore_signal(
            barrier, inc=1, device_id=target, device_id_type=pl.DeviceIdType.MESH
        )
    pl.semaphore_wait(barrier, levels + depths)

    def swap(src, dst, sent_at, landed_at, target):
        return pltpu.make_async_remote_copy(
            src_ref=src, dst_ref=dst, send_sem=sent_at, recv_sem=landed_at,
            device_id=target, device_id_type=pl.DeviceIdType.MESH,
        )

    places = part_ref.shape[0] // 2
    for place in range(places):
        keep[0][place] = part_ref[chunk_of(me, 0, place, levels)]
        send[0][place] = part_ref[chunk_of(me, 1, place, levels)].astype(BF)
    rank = part_ref.shape[1]
    for level in range(levels):
        copy = swap(send[level], land[level], sent.at[level], landed.at[level], other(me, level))
        copy.start()
        copy.wait()
        for place in range(places):
            value = keep[level][place] + land[level][place].astype(F32)
            if level == levels - 1:
                held[0][0, :rank] = value.astype(BF)
            elif place >= places // 2:
                send[level + 1][place - places // 2] = value.astype(BF)
            else:
                keep[level + 1][place] = value
        places //= 2
    held[0][0, rank:] = own_refs[0][...].astype(BF)
    for n in range(1, groups):
        held[n][0] = own_refs[n][...].astype(BF)
    for k in range(depths):
        copies = [
            swap(held[n].at[k], come[n].at[k], far_sent.at[k, n], far_landed.at[k, n], far(z, k))
            for n in range(groups)
        ]
        for copy in copies:
            copy.start()
        for n, copy in enumerate(copies):
            copy.wait()
            value = held[n][k].astype(F32) + come[n][k].astype(F32)
            if k == depths - 1:
                sums[n][...] = value
            else:
                held[n][k + 1] = value.astype(BF)
    for n, (number, upper_at, square_at) in enumerate(ranks):
        square = sums[n][square_at:square_at + 8]
        scale_outs[n][...] = square * inv_refs[n][...]
        betas = square * coef_refs[n][...]
        for i in range(number):
            at = upper_at + i * R
            full[n][me, i * R:(i + 1) * R] = (
                2.0 * (
                    sums[n][at:at + R] - cross_refs[n][i * R:(i + 1) * R] * betas[i:i + 1]
                )
            ).astype(BF)
        full[n][me, number * R:] = jnp.concatenate([betas, jnp.zeros_like(betas)], 0).astype(BF)
    known, serial = [()], 0
    for bit in range(levels - 1, -1, -1):
        copies = []
        for flips in known:
            at = 0
            for k in range(levels):
                mine = bit_of(me, k)
                at = at + ((1 - mine) if k in flips else mine) * (1 << k)
            for n in range(groups):
                copies.append(
                    swap(
                        full[n].at[at], full[n].at[at], full_sent.at[serial, n],
                        full_landed.at[serial, n], other(me, bit),
                    )
                )
            serial += 1
        for copy in copies:
            copy.start()
        for copy in copies:
            copy.wait()
        known = known + [flips + (bit,) for flips in known]
    for load in loads:
        load.wait()
    for n, (group, i, (own_group, own_at)) in enumerate(weights):
        number = ranks[group][0]
        chunks, _, size = full[group].shape
        beta_ref = beta_refs[group]
        for c in range(chunks):
            cols = slice(c * size, (c + 1) * size)
            upper_outs[n][:, cols] = full[group][c, i * R:(i + 1) * R].astype(F32)
            row = full[group][c, number * R:].astype(F32)[i:i + 1]
            beta_ref[:, cols] = jnp.broadcast_to(row, (R, size))
        upper = upper_refs[n][...]
        tilted = (upper * beta_ref[...]).astype(BF)
        core = dot_nt(tilted, upper.astype(BF))
        correction = dot_nt(tilted, bases[n][...]) + 2.0 * dot_nn(
            core.astype(BF), lower_refs[n][...].astype(BF)
        )
        lower_outs[n][...] = 2.0 * (sums[own_group][own_at:own_at + R] - correction)


def reduce_sums(part, groups, weights):
    members = lax.axis_size("mp")
    rank, width = part.shape[0], part.shape[1] // members
    part = jnp.transpose(part.reshape(rank, members, width), (1, 0, 2))
    levels = members.bit_length() - 1
    depths = lax.axis_size("dp").bit_length() - 1
    owns, crosses, coefs, invs, ranks = zip(*groups)
    places, bases, uppers, lowers = zip(*weights)
    shapes = [(rank + owns[0].shape[0], width)] + [v.shape for v in owns[1:]]
    fulls = [(members, r[0] * R + 16, v[1]) for r, v in zip(ranks, shapes)]
    vmem, dma = pl.BlockSpec(memory_space=pltpu.VMEM), pltpu.SemaphoreType.DMA

    def halves(dtype):
        return [pltpu.VMEM((members >> (k + 1), rank, width), dtype) for k in range(levels)]

    steps = [pltpu.VMEM((depths,) + tuple(v), BF) for v in shapes]
    number = len(groups)
    return pl.pallas_call(
        functools.partial(
            reduce_body, levels=levels, depths=depths, ranks=ranks, weights=places
        ),
        in_specs=[
            *[vmem] * (1 + 4 * number),
            *[pl.BlockSpec(memory_space=pl.ANY)] * len(bases),
            *[vmem] * (2 * len(bases)),
        ],
        out_specs=[vmem] * (number + 2 * len(bases)),
        out_shape=[
            *[sds((8, v[1]), F32) for v in shapes],
            *[sds(v.shape, F32) for v in uppers],
            *[sds(v.shape, F32) for v in lowers],
        ],
        scratch_shapes=[
            *halves(F32), *halves(BF), *halves(BF),
            *[pltpu.VMEM(v, F32) for v in shapes], *steps, *steps,
            *[pltpu.VMEM(v, BF) for v in fulls],
            *[pltpu.VMEM((R, members * v[1]), F32) for v in shapes],
            *[pltpu.VMEM(v.shape, BF) for v in bases],
            dma((levels,)), dma((levels,)),
            dma((depths, number)), dma((depths, number)),
            dma((members - 1, number)), dma((members - 1, number)),
            dma((len(bases),)),
        ],
        compiler_params=pltpu.CompilerParams(collective_id=4, has_side_effects=True),
        cost_estimate=estimate(0, 60_000_000),
        name="reduce_sums",
    )(part, *owns, *crosses, *coefs, *invs, *bases, *uppers, *lowers)


def split_low(value):
    high = lax.reduce_precision(value, 8, 7)
    return high, value - high


def block_diagonal(blocks):
    width = sum(b.shape[1] for b in blocks)
    at = 0
    result = []
    for b in blocks:
        result.append(jnp.pad(b, ((0, 0), (at, width - at - b.shape[1]))))
        at += b.shape[1]
    return jnp.concatenate(result, axis=0)


def pad_rows(value, at=0):
    return jnp.pad(value, ((at, RP - at - value.shape[0]), (0, 0))).astype(BF)


def flip(value, bit, axis="mp"):
    size = lax.axis_size(axis)
    return lax.ppermute(value, axis, [(i, i ^ (1 << bit)) for i in range(size)])


def gather_small(value, me):
    part = value[None]
    for bit in range(lax.axis_size("mp").bit_length() - 1):
        came = flip(part, bit)
        upper = ((me >> bit) & 1) == 1
        part = jnp.concatenate(
            [jnp.where(upper, came, part), jnp.where(upper, part, came)], axis=0
        )
    return part


def scatter_cols(value, me):
    members = lax.axis_size("mp")
    part = jnp.transpose(value.reshape(value.shape[0], members, -1), (1, 0, 2))
    for bit in range(members.bit_length() - 1):
        mine = (me >> bit) & 1
        pair = part.reshape(part.shape[0] // 2, 2, *part.shape[1:])
        keep = lax.dynamic_index_in_dim(pair, mine, 1, keepdims=False)
        away = lax.dynamic_index_in_dim(pair, 1 - mine, 1, keepdims=False)
        part = keep + flip(away, bit)
    return part[0]


def tie(value, *others):
    return lax.optimization_barrier((value, *others))[0]


def tables(lengths, length):
    ends = jnp.cumsum(lengths)
    at = jnp.arange(length, dtype=jnp.int32)
    after = (at[:, None] >= ends[None, :NDOC]).astype(jnp.int32)
    segment = jnp.sum(after, axis=1)
    start = jnp.sum(after * lengths[None, :NDOC], axis=1)
    half = jnp.arange(HD // 2, dtype=F32)
    frequency = ROPE_BASE ** (-(2.0 * half / HD))
    angles = (at - start).astype(F32)[:, None] * frequency[None, :]
    cos, sin = jnp.cos(angles), jnp.sin(angles)
    return (
        start,
        (segment < NDOC).astype(F32)[:, None],
        jnp.concatenate([cos, cos], axis=1),
        jnp.concatenate([sin, -sin], axis=1),
    )


def on_device(
    tokens, doc_lengths, out_grad, attn_gain, ffn_gain,
    query_base, query_lower, query_upper, query_scale,
    key_base, key_lower, key_upper, key_scale,
    value_base, value_lower, value_upper, value_scale,
    output_base, output_lower, output_upper, output_scale,
    gate_base, gate_lower, gate_upper, gate_scale,
    lift_base, lift_lower, lift_upper, lift_scale,
    down_base, down_lower, down_upper, down_scale,
):
    members = lax.axis_size("mp")
    me = lax.axis_index("mp")
    seqs, length, width = tokens.shape
    depth = members * width
    hidden = down_base.shape[0]
    block = min(256, length)

    def gather(value):
        return lax.all_gather(value, "mp", axis=0)

    def own_cols(value, size):
        return lax.dynamic_slice_in_dim(value, me * size, size, 1)

    def exchange(value):
        return lax.all_to_all(value, "mp", split_axis=0, concat_axis=0, tiled=True)

    qkv_arranged = arrange([query_base, key_base, value_base], members)
    qkv_base = exchange(qkv_arranged)
    pack = jnp.concatenate(
        [
            tie(query_lower, qkv_arranged).T, key_lower.T, value_lower.T,
            gate_lower.T, lift_lower.T,
            jnp.stack([attn_gain, ffn_gain]),
        ],
        axis=0,
    )
    pack = jnp.pad(pack, ((0, 88 - pack.shape[0]), (0, 0)))
    packed = jnp.transpose(gather_small(pack, me), (1, 0, 2)).reshape(pack.shape[0], depth)
    tok_all = [gather(tokens[s]) for s in range(seqs)]
    lower_qkv_t, lower_gl_t = packed[:3 * R], packed[3 * R:5 * R]
    gain_a, gain_f = packed[5 * R], packed[5 * R + 1]

    output_w, square_o, cross_o = merge(
        tie(output_base, qkv_arranged)[None], output_lower.T, output_upper)
    down_w, square_d, cross_d = merge(
        tie(down_base, qkv_arranged)[None], down_lower.T, down_upper)
    row_stats = scatter_cols(
        jnp.concatenate([square_o, square_d, cross_o, cross_d], axis=0), me
    )
    output_w, down_w = output_w[0], down_w[0]
    norm_o, norm_d = jnp.sqrt(row_stats[0]), jnp.sqrt(row_stats[1])
    cross_o, cross_d = row_stats[2:2 + R], row_stats[2 + R:2 + 2 * R]
    ratio_o, ratio_d = output_scale / norm_o, down_scale / norm_d
    layouts = [tables(doc_lengths[s], length) for s in range(seqs)]
    grad_tops = [out_grad[s].astype(F32) * layouts[s][1] for s in range(seqs)]
    gd_low = [(grad_tops[s] * ratio_d).astype(BF) for s in range(seqs)]
    gd_all = [gather(gd_low[s]) for s in range(seqs)]

    upper_qkv = block_diagonal([own_cols(u, width) for u in (query_upper, key_upper, value_upper)])
    upper_g, upper_l = own_cols(gate_upper, hidden), own_cols(lift_upper, hidden)
    qkv_w, square_qkv, cross_all = merge(qkv_base, lower_qkv_t, upper_qkv)
    qkv_w = qkv_w.reshape(depth, 3 * width)
    norm_qkv = jnp.sqrt(square_qkv[0])
    scale_qkv = jnp.concatenate([query_scale, key_scale, value_scale])
    ratio_qkv = (scale_qkv / norm_qkv)[None]
    inv_ratio = 1.0 / ratio_qkv

    gl_arranged = arrange([gate_base, lift_base], members)
    gl_base = exchange(tie(gl_arranged, tok_all[0]))
    gate_w, lift_w, square_gl, cross_g, cross_l = merge(
        gl_base, lower_gl_t, block_diagonal([upper_g, upper_l]), [hidden, hidden]
    )
    gate_w, lift_w = gate_w.reshape(depth, hidden), lift_w.reshape(depth, hidden)
    norm_gl = jnp.sqrt(square_gl[0])
    norm_g, norm_l = norm_gl[:hidden], norm_gl[hidden:]
    ratio_g, ratio_l = (gate_scale / norm_g)[None], (lift_scale / norm_l)[None]

    low_l_qkv, low_l_gl = pad_rows(lower_qkv_t), pad_rows(lower_gl_t)
    low_u_qkv, low_u_g, low_u_l = pad_rows(upper_qkv), pad_rows(upper_g), pad_rows(upper_l, R)
    low_l_d, low_u_d = pad_rows(down_lower.T).T, pad_rows(down_upper)
    low_l_o, low_u_o = pad_rows(output_lower.T).T, pad_rows(output_upper)
    chunk_gain_a, chunk_gain_f = (v.reshape(members, 1, width) for v in (gain_a, gain_f))

    state = [dict() for _ in range(seqs)]

    def attention_stage(s):
        st = state[s]
        start, _, st["cos"], st["sin"] = layouts[s]
        st["start"] = start.reshape(length // block, block)
        st["lo"] = st["start"][:, 0] // block
        if s == 0:
            tok = tie(tok_all[s], gl_arranged, *gd_low)
        else:
            tok = tie(tok_all[s], state[s - 1]["residual_low"])
        st["x"], st["y"], st["q"], st["k"], st["xl"], st["inv"] = qkv_forward(
            tok, chunk_gain_a, qkv_w, low_l_qkv, ratio_qkv, st["cos"], st["sin"]
        )
        st["att"], st["lse"] = attend_forward(
            st["lo"], st["start"], st["q"], st["k"], st["y"], block
        )
        act = tie(st["att"], gate_w, lift_w) if s == seqs - 1 else st["att"]
        st["inner_o"] = out_forward(act, output_w).astype(F32)
        st["residual"] = tokens[s].astype(F32) + st["inner_o"] * ratio_o
        st["residual_low"] = st["residual"].astype(BF)
        st["residual_all"] = gather(st["residual_low"])

    def ffn_stage(s):
        st = state[s]
        if s + 1 < seqs:
            res = tie(st["residual_all"], state[s + 1]["residual_low"])
        else:
            res = tie(st["residual_all"], state[s - 1]["grad_output_low"])
        st["inner_d"], back, st["inv_f"], dot_f, *st["ffn"] = ffn(
            res, chunk_gain_f, gd_all[s], gate_w, lift_w, down_w,
            ratio_g, ratio_l, low_l_gl, low_u_g, low_u_l, low_l_d, low_u_d,
        )
        inv = st["inv_f"]
        grad_residual = (
            grad_tops[s] + inv * (ffn_gain * back.astype(F32))
            - st["residual"] * (inv * inv * dot_f / depth)
        )
        st["grad_residual"] = grad_residual
        st["grad_output_low"] = (grad_residual * ratio_o).astype(BF)
        st["grad_output"] = gather(st["grad_output_low"])
        inner_d = st["inner_d"].astype(F32)
        st["out"] = (st["residual"] + inner_d * ratio_d).astype(BF)
        st["g_d"] = jnp.sum(inner_d * grad_tops[s], axis=0)
        st["g_o"] = jnp.sum(st["inner_o"] * grad_residual, axis=0)

    def attention_back_stage(s):
        st = state[s]
        grad = st["grad_output"]
        if s + 1 < seqs:
            grad = tie(grad, state[s + 1]["grad_output_low"])
        else:
            grad = tie(grad, state[s - 1]["dx"])
        grad_att, st["a_o"], st["b_o"] = out_back(
            grad, st["att"], output_w, low_u_o, low_l_o
        )
        grads = attend_backward(
            st["lo"], st["start"], st["q"], st["k"], st["y"], grad_att, st["att"],
            st["lse"], st["cos"], st["sin"], ratio_qkv, block,
        )
        st["dx"], dot_a, st["a_qkv"], st["b_qkv"], st["g_qkv"] = qkv_backward(
            grads, st["y"], st["x"], st["xl"], qkv_w, low_u_qkv, inv_ratio, members
        )
        inv = st["inv"]
        st["in_grad"] = (
            st["grad_residual"] + inv * (attn_gain * st["dx"].astype(F32))
            - tokens[s].astype(F32) * (inv * inv * dot_a / depth)
        )

    for stage in (attention_stage, ffn_stage, attention_back_stage):
        for s in range(seqs):
            stage(s)

    out_tokens = jnp.stack([st["out"] for st in state])
    in_grad = jnp.stack([st["in_grad"] for st in state])

    def total(pick):
        result = pick(state[0])
        for s in range(1, seqs):
            result = result + pick(state[s])
        return result

    def blocks_of(value, size):
        return jnp.concatenate(
            [value[n * R:(n + 1) * R, n * size:(n + 1) * size] for n in range(value.shape[0] // R)],
            axis=0,
        )

    def stacked(values, height):
        value = jnp.concatenate(values, axis=0)
        return jnp.pad(value, ((0, height - value.shape[0]), (0, 0)))

    coef_qkv = (scale_qkv / norm_qkv ** 3).reshape(3, width)
    coef_o, coef_d = output_scale / norm_o ** 3, down_scale / norm_d ** 3
    coef_g, coef_l = gate_scale / norm_g ** 3, lift_scale / norm_l ** 3
    norm_rows = norm_qkv.reshape(3, width)
    groups = [
        (
            stacked(
                [
                    blocks_of(total(lambda st: st["b_qkv"])[:3 * R], width),
                    total(lambda st: st["a_o"])[:R],
                    total(lambda st: st["g_o"])[None],
                    total(lambda st: st["g_d"])[None],
                    total(lambda st: st["g_qkv"]).reshape(3, width),
                ],
                4 * R + 8,
            ),
            jnp.concatenate([cross_o, cross_d, blocks_of(cross_all, width)], axis=0),
            stacked([coef_o[None], coef_d[None], coef_qkv], 8),
            stacked([1.0 / norm_o[None], 1.0 / norm_d[None], 1.0 / norm_rows], 8),
            (5, 5 * R, 11 * R),
        ),
        (
            stacked(
                [
                    total(lambda st: st["ffn"][1])[:R],
                    total(lambda st: st["ffn"][2])[R:2 * R],
                    total(lambda st: st["ffn"][3])[:R],
                    total(lambda st: st["ffn"][5]),
                    total(lambda st: st["ffn"][6]),
                ],
                3 * R + 8,
            ),
            jnp.concatenate([cross_g[:R], cross_l[R:2 * R]], axis=0),
            stacked([coef_g[None], coef_l[None]], 8),
            stacked([1.0 / norm_g[None], 1.0 / norm_l[None]], 8),
            (2, 0, 3 * R),
        ),
    ]
    weights = [
        ((0, 2, (0, 0)), query_base, query_upper, query_lower.T),
        ((0, 3, (0, R)), key_base, key_upper, key_lower.T),
        ((0, 4, (0, 2 * R)), value_base, value_upper, value_lower.T),
        ((0, 0, (0, 10 * R)), output_base, output_upper, output_lower.T),
        ((1, 0, (0, 3 * R)), gate_base, gate_upper, gate_lower.T),
        ((1, 1, (0, 4 * R)), lift_base, lift_upper, lift_lower.T),
        ((0, 1, (1, 2 * R)), down_base, down_upper, down_lower.T),
    ]
    part = jnp.concatenate(
        [
            total(lambda st: st["a_qkv"])[:3 * R],
            total(lambda st: st["ffn"][0])[:2 * R],
            total(lambda st: st["b_o"])[:R],
            total(lambda st: st["ffn"][4])[:R],
        ],
        axis=0,
    )
    finished = reduce_sums(part, groups, weights)
    results = [out_tokens, in_grad]
    for n, ((group, i, _), _, _, _) in enumerate(weights):
        results += [finished[2 + len(weights) + n].T, finished[2 + n], finished[group][i]]
    return tuple(results)


def solution(mesh):
    spread, split, rows_spec = P("dp", None, "mp"), P("mp"), P("mp", None)
    weight = (rows_spec, rows_spec, P(), split)
    grads = (rows_spec, P(), split)

    return jax.shard_map(
        on_device,
        mesh=mesh,
        in_specs=(spread, P("dp", None), spread, split, split) + weight * 7,
        out_specs=(spread, spread) + grads * 7,
        check_vma=False,
    )
```

profile of v0, /device:TPU:0, one launch (start us, length us, event | category | flops | bytes accessed | tf_op | source)
XLA Modules:
  0.0 984.7 jit_solution(11211909038468651644)
XLA Ops:
  7.2 3.0 fusion.55
  11.0 3.1 arrange.3
  14.2 5.3 all-to-all-start
  22.1 3.0 merge.5
  27.8 4.6 merge.6
  37.3 3.6 concatenate.107
  47.5 9.2 multiply_sine_fusion
  56.7 1.9 pad_maximum_fusion.2
  58.7 4.8 arrange.2
  65.4 2.0 collective-permute-start.4
  68.3 2.9 collective-permute-done.4
  72.7 2.5 collective-permute-start.1
  76.3 7.4 collective-permute-done.1
  85.3 15.9 %collective-permute-done.2 = f32[4,88,256]{2,1,0:T(8,128)S(1)} collective-permute-done((f32[4,88,256]{2,1,0:T(8,128)S(1)}, f32[4,88,256]{2,1,0:T(8,128)S(1)}, u32[]{:S(2)}, u32[]{:S(2)}) %collective-permute-start.2) | collective-permute-done | bytes 360480 | tf_op jit(solution)/shard_map/ppermute | solution.py:999
  104.0 1.7 copy-done.6
  105.7 7.7 merge.4
  114.8 15.9 %qkv_forward.2 = (bf16[2048,2048]{1,0:T(8,128)(2,1)}, bf16[2048,768]{1,0:T(8,128)(2,1)}, bf16[2048,256]{1,0:T(8,128)(2,1)}, bf16[2048,256]{1,0:T(8,128)(2,1)}, b...) custom-call(bf16[8,2048,256]{2,1,0:T(8,128)(2,1)} %all-gather.13.cloned.1.call-done.tok_ref, ...), custom_call_target="tpu_custom_call" | custom-call | flops 7516192768 | bytes 25165824 | tf_op jit(solution)/shard_map/qkv_forward/pallas_call | solution.py:339
  130.7 20.3 %attend_forward.2 = (bf16[2048,256]{1,0:T(8,128)(2,1)}, f32[2,8,256]{2,1,0:T(8,128)}) custom-call(s32[8]{0:T(128)} %get-tuple-element.321.lo_ref, s32[8,256]{1,0:T(8,128)} %copy-done.43, bf16[2048,256]{1,0:T(8,128)(2,1)} %get-tuple-element.122.q_ref, bf16[2048,256]{1,0:T(8,128)(2,1)} %get-tuple-element.123.k_ref, ...), custom_call_target="tpu_custom_call" | custom-call | flops 2147483648 | bytes 4194304 | tf_op jit(solution)/shard_map/attend_forward/pallas_call | solution.py:427
  150.9 53.7 %out_forward.2 = bf16[2048,256]{1,0:T(8,128)(2,1)} custom-call(bf16[2048,256]{1,0:T(8,128)(2,1)} %get-tuple-element.125.a_ref.o_ref, bf16[256,2048]{1,0:T(8,128)(2,1)} %bitcast.230), custom_call_target="tpu_custom_call" | custom-call | flops 2147483648 | bytes 167772160 | tf_op jit(solution)/shard_map/out_forward/pallas_call | solution.py:579
  204.7 2.6 fusion.22
  208.2 3.0 fusion.11
  211.2 4.9 all-to-all-start.1
  217.9 3.8 pad_maximum_fusion.4
  224.2 15.9 %qkv_forward.3 = (bf16[2048,2048]{1,0:T(8,128)(2,1)}, bf16[2048,768]{1,0:T(8,128)(2,1)}, bf16[2048,256]{1,0:T(8,128)(2,1)}, bf16[2048,256]{1,0:T(8,128)(2,1)}, b...) custom-call(bf16[8,2048,256]{2,1,0:T(8,128)(2,1)} %all-gather.15.cloned.1.call-done.tok_ref, ...), custom_call_target="tpu_custom_call" | custom-call | flops 7516192768 | bytes 25165824 | tf_op jit(solution)/shard_map/qkv_forward/pallas_call | solution.py:339
  240.1 20.8 %attend_forward.3 = (bf16[2048,256]{1,0:T(8,128)(2,1)}, f32[2,8,256]{2,1,0:T(8,128)}) custom-call(s32[8]{0:T(128)} %get-tuple-element.320.lo_ref, s32[8,256]{1,0:T(8,128)} %copy-done.42, bf16[2048,256]{1,0:T(8,128)(2,1)} %get-tuple-element.134.q_ref, bf16[2048,256]{1,0:T(8,128)(2,1)} %get-tuple-element.135.k_ref, ...), custom_call_target="tpu_custom_call" | custom-call | flops 2147483648 | bytes 4194304 | tf_op jit(solution)/shard_map/attend_forward/pallas_call | solution.py:427
  260.9 53.9 %all-to-all-done.1.base_ref = bf16[8,256,1408]{2,1,0:T(8,128)(2,1)} async-done(((bf16[8,256,1408]{2,1,0:T(8,128)(2,1)}), bf16[8,256,1408]{2,1,0:T(8,128)(2,1)}, u32[]{:S(2)}, u32[]{:S(2)}) %all-to-all-start.1) | async-done | bytes 5767200 | tf_op jit(solution)/shard_map/all_to_all | solution.py:1071
  314.8 9.0 merge.7
  323.8 79.8 %out_forward.3 = bf16[2048,256]{1,0:T(8,128)(2,1)} custom-call(bf16[2048,256]{1,0:T(8,128)(2,1)} %get-tuple-element.141.a_ref.o_ref, bf16[256,2048]{1,0:T(8,128)(2,1)} %bitcast.231), custom_call_target="tpu_custom_call" | custom-call | flops 2147483648 | bytes 167772160 | tf_op jit(solution)/shard_map/out_forward/pallas_call | solution.py:579
  403.6 2.6 fusion.23
  412.2 140.3 %ffn.2 = (bf16[2048,256]{1,0:T(8,128)(2,1)}, bf16[2048,256]{1,0:T(8,128)(2,1)}, f32[2048,1]{1,0:T(8,128)}, f32[2048,1]{1,0:T(8,128)}, f32[128,2048]{1,0:T(8,128)...) custom-call(bf16[8,2048,256]{2,1,0:T(8,128)(2,1)} %bitcast.216, ...), custom_call_target="tpu_custom_call" | custom-call | flops 41339060224 | bytes 167772160 | tf_op jit(solution)/shard_map/ffn/pallas_call | solution.py:674
  552.6 2.3 fusion.50
  554.9 2.9 fusion
  560.3 8.7 all-gather.27.cloned.1.call-start
  569.0 117.8 %ffn.3 = (bf16[2048,256]{1,0:T(8,128)(2,1)}, bf16[2048,256]{1,0:T(8,128)(2,1)}, f32[2048,1]{1,0:T(8,128)}, f32[2048,1]{1,0:T(8,128)}, f32[128,2048]{1,0:T(8,128)...) custom-call(bf16[8,2048,256]{2,1,0:T(8,128)(2,1)} %bitcast.219, ...), custom_call_target="tpu_custom_call" | custom-call | flops 41339060224 | bytes 167772160 | tf_op jit(solution)/shard_map/ffn/pallas_call | solution.py:674
  686.9 2.3 fusion.49
  689.2 6.0 fusion.1
  713.3 2.7 pad_maximum_fusion.1
  718.1 12.4 %out_back.2 = (bf16[2048,256]{1,0:T(8,128)(2,1)}, f32[128,256]{1,0:T(8,128)}, f32[128,2048]{1,0:T(8,128)}) custom-call(bf16[8,2048,256]{2,1,0:T(8,128)(2,1)} %bitcast.217, bf16[2048,256]{1,0:T(8,128)(2,1)} %get-tuple-element.125.a_ref.o_ref, bf16[256,2048]{1,0:T(8,128)(2,1)} %bitcast.232, bf16[128,2048]{1,0:T(8,128)(2,1)} %pad.101.u_ref, ...), custom_call_target="tpu_custom_call" | custom-call | flops 4294967296 | bytes 12582912 | tf_op jit(solution)/shard_map/out_back/pallas_call | solution.py:726
  730.6 24.1 %attend_backward.2.g_ref = bf16[2048,768]{1,0:T(8,128)(2,1)} custom-call(s32[8]{0:T(128)} %get-tuple-element.321.lo_ref, s32[8,256]{1,0:T(8,128)} %copy-done.43, bf16[2048,256]{1,0:T(8,128)(2,1)} %get-tuple-element.122.q_ref, bf16[2048,256]{1,0:T(8,128)(2,1)} %get-tuple-element.123.k_ref, bf16[2048,768]{1,0:T(8,128)(2,1)} %get-tuple-element.124.v_ref.y_ref, ...), custom_call_target="tpu_custom_call" | custom-call | flops 5368709120 | bytes 8388608 | tf_op jit(solution)/shard_map/attend_backward/pallas_call | solution.py:526
  754.7 56.7 %qkv_backward.2 = (bf16[2048,256]{1,0:T(8,128)(2,1)}, f32[2048,1]{1,0:T(8,128)}, f32[128,2048]{1,0:T(8,128)}, f32[128,768]{1,0:T(8,128)}, f32[1,768]{1,0:T(1,128)}) custom-call(bf16[2048,768]{1,0:T(8,128)(2,1)} %attend_backward.2.g_ref, bf16[2048,768]{1,0:T(8,128)(2,1)} %get-tuple-element.124.v_ref.y_ref, bf16[2048,2048]{1,0:T(8,128)(2,1)} %get-tuple-element.158.x_ref, ...), custom_call_target="tpu_custom_call" | custom-call | flops 12884901888 | bytes 167772160 | tf_op jit(solution)/shard_map/qkv_backward/pallas_call | solution.py:778
  811.4 1.8 fusion.47
  813.3 12.2 %out_back.3 = (bf16[2048,256]{1,0:T(8,128)(2,1)}, f32[128,256]{1,0:T(8,128)}, f32[128,2048]{1,0:T(8,128)}) custom-call(bf16[8,2048,256]{2,1,0:T(8,128)(2,1)} %bitcast.218, bf16[2048,256]{1,0:T(8,128)(2,1)} %get-tuple-element.141.a_ref.o_ref, bf16[256,2048]{1,0:T(8,128)(2,1)} %bitcast.233, bf16[128,2048]{1,0:T(8,128)(2,1)} %pad.101.u_ref, ...), custom_call_target="tpu_custom_call" | custom-call | flops 4294967296 | bytes 12582912 | tf_op jit(solution)/shard_map/out_back/pallas_call | solution.py:726
  825.5 24.5 %attend_backward.3.g_ref = bf16[2048,768]{1,0:T(8,128)(2,1)} custom-call(s32[8]{0:T(128)} %get-tuple-element.320.lo_ref, s32[8,256]{1,0:T(8,128)} %copy-done.42, bf16[2048,256]{1,0:T(8,128)(2,1)} %get-tuple-element.134.q_ref, bf16[2048,256]{1,0:T(8,128)(2,1)} %get-tuple-element.135.k_ref, bf16[2048,768]{1,0:T(8,128)(2,1)} %get-tuple-element.136.v_ref.y_ref, ...), custom_call_target="tpu_custom_call" | custom-call | flops 5368709120 | bytes 8388608 | tf_op jit(solution)/shard_map/attend_backward/pallas_call | solution.py:526
  850.0 57.6 %qkv_backward.3 = (bf16[2048,256]{1,0:T(8,128)(2,1)}, f32[2048,1]{1,0:T(8,128)}, f32[128,2048]{1,0:T(8,128)}, f32[128,768]{1,0:T(8,128)}, f32[1,768]{1,0:T(1,128)}) custom-call(bf16[2048,768]{1,0:T(8,128)(2,1)} %attend_backward.3.g_ref, bf16[2048,768]{1,0:T(8,128)(2,1)} %get-tuple-element.136.v_ref.y_ref, bf16[2048,2048]{1,0:T(8,128)(2,1)} %get-tuple-element.166.x_ref, ...), custom_call_target="tpu_custom_call" | custom-call | flops 12884901888 | bytes 167772160 | tf_op jit(solution)/shard_map/qkv_backward/pallas_call | solution.py:778
  914.0 43.1 %reduce_sums.1 = (f32[8,256]{1,0:T(8,128)}, f32[8,704]{1,0:T(8,128)}, f32[16,2048]{1,0:T(8,128)}, f32[16,2048]{1,0:T(8,128)}, f32[16,2048]{1,0:T(8,128)}, /*inde...) custom-call(f32[8,112,256]{2,1,0:T(8,128)} %bitcast.173, ...), custom_call_target="tpu_custom_call" | custom-call | bytes 60000000 | tf_op jit(solution)/shard_map/reduce_sums/pallas_call | solution.py:946
  960.2 2.1 fusion.48
  962.3 3.6 fusion.19
  966.1 2.3 pad_maximum_fusion
  (312 shorter events, 80.8 us)
Async XLA Ops:
  7.2 107.6 %all-gather.13.cloned.1.call-start = ((), (), s32[]{:S(2)}) async-start(), calls=%async_computation.2 | async-start | bytes 9437184 | tf_op jit(solution)/shard_map/all_gather | solution.py:1065
  10.3 213.9 %all-gather.15.cloned.1.call-start = ((), (), s32[]{:S(2)}) async-start(), calls=%async_computation.3 | async-start | bytes 9437184 | tf_op jit(solution)/shard_map/all_gather | solution.py:1065
  14.2 6.6 copy-start.16
  14.2 11.0 %copy-start.18 = (f32[704,16]{0,1:T(8,128)S(1)}, f32[704,16]{0,1:T(8,128)}, u32[]{:S(2)}) copy-start(f32[704,16]{0,1:T(8,128)} %param.63) | copy-start | bytes 135172
  14.2 89.9 %all-to-all-start = ((bf16[8,256,768]{2,1,0:T(8,128)(2,1)}), bf16[8,256,768]{2,1,0:T(8,128)(2,1)S(1)}, u32[]{:S(2)}, u32[]{:S(2)}) async-start(bf16[8,256,768]{2,1,0:T(8,128)(2,1)} %arrange.3), calls=%async_computation | async-start | bytes 6291456 | tf_op jit(solution)/shard_map/all_to_all | solution.py:1071
  19.5 6.9 copy-start.17
  19.5 392.7 %all-gather.21.cloned.1.call-start = ((), (), s32[]{:S(2)}) async-start(), calls=%async_computation.6 | async-start | bytes 9437184 | tf_op jit(solution)/shard_map/all_gather | solution.py:1065
  26.4 5.9 copy-start.28
  36.9 27.3 %collective-permute-start.3 = (f32[4,34,256]{2,0,1:T(4,128)}, f32[4,34,256]{2,0,1:T(4,128)}, u32[]{:S(2)}, u32[]{:S(2)}) collective-permute-start(f32[4,34,256]{2,0,1:T(4,128)} %bitcast.168), channel_id=1, source_target_pairs={{0,1},{1,0},{2,3},{3,2},{4,5},{5,4},{6,7},{7,6},{8,9},{9,8},{10,11... | collective-permute-start | bytes 417800 | tf_op jit(solution)/shard_map/ppermute | solution.py:999
  41.5 25.9 %collective-permute-start = (f32[1,88,256]{2,1,0:T(8,128)}, f32[1,88,256]{2,1,0:T(8,128)}, u32[]{:S(2)}, u32[]{:S(2)}) collective-permute-start(f32[1,88,256]{2,1,0:T(8,128)} %pad_bitcast_fusion.1), channel_id=1, source_target_pairs={{0,1},{1,0},{2,3},{3,2},{4,5},{5,4},{6,7},{7,6},{8,9},{9,8},{10,11... | collective-permute-start | bytes 270344 | tf_op jit(solution)/shard_map/ppermute | solution.py:999
  46.9 11.7 %copy-start.26 = (f32[16,256]{1,0:T(8,128)}, f32[16,256]{1,0:T(8,128)S(1)}, u32[]{:S(2)}) copy-start(f32[16,256]{1,0:T(8,128)S(1)} %get-tuple-element.323) | copy-start | bytes 49156
  58.6 5.5 copy-start.15
  65.3 19.5 %copy-start.65 = (f32[256]{0:T(256)S(1)}, f32[256]{0:T(256)}, u32[]{:S(2)}) copy-start(f32[256]{0:T(256)} %param.53) | copy-start | bytes 3076
  65.4 5.8 collective-permute-start.4
  71.3 5.1 collective-permute-start.5
  72.7 11.0 %collective-permute-start.1 = (f32[2,88,256]{2,1,0:T(8,128)S(1)}, f32[2,88,256]{2,1,0:T(8,128)S(1)}, u32[]{:S(2)}, u32[]{:S(2)}) collective-permute-start(f32[2,88,256]{2,1,0:T(8,128)S(1)} %pad_maximum_fusion.15), channel_id=1, source_target_pairs={{0,2},{1,3},{2,0},{3,1},{4,6},{5,7},{6,4},{7,5},{8,10},{9,11},{10,... | collective-permute-start | bytes 540680 | tf_op jit(solution)/shard_map/ppermute | solution.py:999
  83.8 17.4 %collective-permute-start.2 = (f32[4,88,256]{2,1,0:T(8,128)S(1)}, f32[4,88,256]{2,1,0:T(8,128)S(1)}, u32[]{:S(2)}, u32[]{:S(2)}) collective-permute-start(f32[4,88,256]{2,1,0:T(8,128)S(1)} %pad_maximum_fusion.9), channel_id=1, source_target_pairs={{0,4},{1,5},{2,6},{3,7},{4,0},{5,1},{6,2},{7,3},{8,12},{9,13},{10,... | collective-permute-start | bytes 1081352 | tf_op jit(solution)/shard_map/ppermute | solution.py:999
  104.0 9.4 copy-start.60
  104.0 9.4 copy-start.62
  104.0 9.4 copy-start.63
  150.9 53.7 %copy-start = (bf16[2,2048,256]{2,1,0:T(8,128)(2,1)S(1)}, bf16[2,2048,256]{2,1,0:T(8,128)(2,1)}, u32[]{:S(2)}) copy-start(bf16[2,2048,256]{2,1,0:T(8,128)(2,1)} %param.33) | copy-start | bytes 6291460
  207.3 204.9 %all-gather.17.cloned.1.call-start = ((), (), s32[]{:S(2)}) async-start(), calls=%async_computation.4 | async-start | bytes 9437184 | tf_op jit(solution)/shard_map/all_gather | solution.py:1065
  211.2 6.7 copy-start.8
  211.2 103.6 %all-to-all-start.1 = ((bf16[8,256,1408]{2,1,0:T(8,128)(2,1)}), bf16[8,256,1408]{2,1,0:T(8,128)(2,1)}, u32[]{:S(2)}, u32[]{:S(2)}) async-start(bf16[8,256,1408]{2,1,0:T(8,128)(2,1)} %arrange.2), calls=%async_computation.1 | async-start | bytes 11534336 | tf_op jit(solution)/shard_map/all_to_all | solution.py:1071
  216.1 352.9 %all-gather.23.cloned.1.call-start = ((), (), s32[]{:S(2)}) async-start(), calls=%async_computation.7 | async-start | bytes 9437184 | tf_op jit(solution)/shard_map/all_gather | solution.py:1065
  406.2 5.4 copy-start.59
  406.2 162.8 %all-gather.19.cloned.1.call-start = ((), (), s32[]{:S(2)}) async-start(), calls=%async_computation.5 | async-start | bytes 9437184 | tf_op jit(solution)/shard_map/all_gather | solution.py:1065
  406.8 311.3 %all-gather.25.cloned.1.call-start = ((), (), s32[]{:S(2)}) async-start(), calls=%async_computation.8 | async-start | bytes 9437184 | tf_op jit(solution)/shard_map/all_gather | solution.py:1065
  412.2 142.7 %copy-start.7 = (bf16[2048,256]{1,0:T(8,128)(2,1)S(1)}, bf16[2048,256]{1,0:T(8,128)(2,1)}, u32[]{:S(2)}) copy-start(bf16[2048,256]{1,0:T(8,128)(2,1)} %out_forward.2) | copy-start | bytes 3145732
  560.3 253.0 %all-gather.27.cloned.1.call-start = ((), (), s32[]{:S(2)}) async-start(), calls=%async_computation.9 | async-start | bytes 9437184 | tf_op jit(solution)/shard_map/all_gather | solution.py:1065
  696.5 7.8 copy-start.40
  697.7 6.5 copy-start.41
  697.7 15.6 %copy-start.9 = (bf16[1,2048,256]{2,1,0:T(8,128)(2,1)S(1)}, bf16[1,2048,256]{2,1,0:T(8,128)(2,1)}, u32[]{:S(2)}) copy-start(bf16[1,2048,256]{2,1,0:T(8,128)(2,1)} %get-tuple-element.243) | copy-start | bytes 3145732
  754.7 56.7 %copy-start.14 = (f32[2048,1]{1,0:T(8,128)S(1)}, f32[2048,1]{1,0:T(8,128)}, u32[]{:S(2)}) copy-start(f32[2048,1]{1,0:T(8,128)} %get-tuple-element.151) | copy-start | bytes 24580
  850.0 57.6 %copy-start.64 = (f32[1,768]{1,0:T(1,128)S(1)}, f32[1,768]{1,0:T(1,128)}, u32[]{:S(2)}) copy-start(f32[1,768]{1,0:T(1,128)} %get-tuple-element.182) | copy-start | bytes 9220
  850.0 58.3 %copy-start.19 = (f32[128,768]{1,0:T(8,128)S(1)}, f32[128,768]{1,0:T(8,128)}, u32[]{:S(2)}) copy-start(f32[128,768]{1,0:T(8,128)} %get-tuple-element.178) | copy-start | bytes 1179652
  850.0 60.1 %copy-start.54 = (f32[256]{0:T(256)S(1)}, f32[256]{0:T(256)}, u32[]{:S(2)}) copy-start(f32[256]{0:T(256)} %add.199) | copy-start | bytes 3076
  850.0 60.1 %copy-start.55 = (f32[256]{0:T(256)S(1)}, f32[256]{0:T(256)}, u32[]{:S(2)}) copy-start(f32[256]{0:T(256)} %add.197) | copy-start | bytes 3076
  914.0 48.3 %copy-start.13 = (bf16[2048,256]{1,0:T(8,128)(2,1)S(1)}, bf16[2048,256]{1,0:T(8,128)(2,1)}, u32[]{:S(2)}) copy-start(bf16[2048,256]{1,0:T(8,128)(2,1)} %get-tuple-element.160) | copy-start | bytes 3145732
  966.0 5.5 copy-start.31
  966.0 6.1 copy-start.46
  966.0 6.7 copy-start.30
  966.0 7.4 copy-start.45
  966.0 8.0 copy-start.21
  966.1 8.7 copy-start.44
  968.3 7.0 copy-start.20
  968.3 7.8 copy-start.37
  968.4 8.4 copy-start.29
  (35 other events, 114.9 us)
Sparse Core Ops, SparseCore 0:
  10.5 92.4 all-gather.12
  104.9 53.8 all-gather.14
  207.4 103.9 all-gather.20
  313.1 80.7 all-gather.16
  406.3 74.9 all-gather.22
  483.1 75.6 all-gather.18
  560.7 74.6 all-gather.24
  697.9 54.4 all-gather.26
where the time goes:
time: 996 us; the launch traced here: 985 us
  Pallas kernels  727 us (73%)
  other arithmetic  86.3 us (9%)
  waiting for transfers between devices  82.5 us (8%)
  local copies, waits for them, and re-layouts  46 us (5%)
  starting transfers between devices  26.8 us (3%)
  between operations  15.6 us (2%)
    pallas_call x2, Pallas kernels, ffn(): pl.pallas_call(ffn_body, grid=(blocks + levels,), in_specs=[chunk_upto(bl...  258 us
    pallas_call x2, Pallas kernels, out_forward(): pl.pallas_call(out_body, grid=(blocks + levels,), in_specs=[upto(blocks -...  133 us
    pallas_call x2, Pallas kernels, qkv_backward(): pl.pallas_call(qkv_back_body, grid=(blocks + levels,), in_specs=[upto(blo...  114 us
    all_to_all x2, waiting for transfers between devices, exchange(): return lax.all_to_all(value, 'mp', split_axis=0, concat_axis=0, tiled=True)  53.9 us
    pallas_call x2, Pallas kernels, attend_backward(): pl.pallas_call(functools.partial(attend_back_body, block=block), grid=(1,...  48.7 us
    pallas_call x1, Pallas kernels, reduce_sums(): pl.pallas_call(functools.partial(reduce_body, levels=levels, depths=depth...  43.1 us
    pallas_call x2, Pallas kernels, attend_forward(): pl.pallas_call(functools.partial(attend_body, block=block), grid=(1,), in...  41.1 us
    pallas_call x2, Pallas kernels, qkv_forward(): pl.pallas_call(qkv_body, grid=(length // block,), in_specs=[chunk_rows(co...  31.7 us
  transfers between devices with their start and end apart: 16, of which 5 were waited for; matrix products, arithmetic and copies ran while one was open for 10% of the time, Pallas kernels for 60%

commit v1 on v0

--- a/solution.py
+++ b/solution.py
@@ -51,6 +51,10 @@
 
 def estimate(flops, bytes_accessed):
     return pl.CostEstimate(flops=int(flops), bytes_accessed=int(bytes_accessed), transcendentals=0)
+
+
+def smem():
+    return pl.BlockSpec(memory_space=pltpu.SMEM)
 
 
 def bit_of(me, k):
@@ -243,10 +247,10 @@
 def arrange(values, count):
     height = values[0].shape[0]
     size = sum(v.shape[1] for v in values) // count
-    block = height // 2
+    block = max(16, height // 2)
     return pl.pallas_call(
         arrange_body,
-        grid=(2,),
+        grid=(height // block,),
         in_specs=[rows(block, v.shape[1]) for v in values],
         out_specs=chunk_rows(count, block, size),
         out_shape=sds((count, height, size), BF),
@@ -255,7 +259,8 @@
     )(*values)
 
 
-def merge_body(base_ref, l3_ref, u3_ref, l_ref, *refs):
+def merge_body(place_ref, *refs, pieces):
+    base_refs, (l3_ref, u3_ref, l_ref), refs = refs[:pieces], refs[pieces:pieces + 3], refs[pieces + 3:]
     splits = (len(refs) - 1) // 2
     w_refs, square_ref, cross_refs = refs[:splits], refs[splits], refs[splits + 1:]
 
@@ -264,7 +269,14 @@
         for ref in (square_ref, *cross_refs):
             ref[...] = jnp.zeros_like(ref)
 
-    value = base_ref[0].astype(F32) + dot_tn(l3_ref[...], u3_ref[...])
+    parts, place = (pieces + 1) // 2, place_ref[0]
+    base = []
+    for part in range(parts):
+        piece = base_refs[parts - 1 + part][0]
+        for at in range(1, parts):
+            piece = jnp.where(place == at, base_refs[parts - 1 + part - at][0], piece)
+        base.append(piece)
+    value = jnp.concatenate(base, axis=0).astype(F32) + dot_tn(l3_ref[...], u3_ref[...])
     low = value.astype(BF)
     at = 0
     for ref, cross_ref in zip(w_refs, cross_refs):
@@ -274,19 +286,22 @@
     square_ref[...] += jnp.sum(value * value, axis=0, keepdims=True)
 
 
-def merge(base, lower_t, upper, splits=None):
-    count, height, width = base.shape
+def merge(pieces, lower_t, upper, splits=None):
+    count, share, width = pieces[0].shape
+    height = share * ((len(pieces) + 1) // 2)
     splits = splits or [width]
     rank = lower_t.shape[0]
     lower_high, lower_low = split_low(lower_t)
     upper_high, upper_low = split_low(2.0 * upper)
     l3 = jnp.concatenate([lower_high, lower_low, lower_high], axis=0).astype(BF)
     u3 = jnp.concatenate([upper_high, upper_high, upper_low], axis=0).astype(BF)
+    place = jnp.full((1,), lax.axis_index("dp"), jnp.int32)
     return pl.pallas_call(
-        merge_body,
+        functools.partial(merge_body, pieces=len(pieces)),
         grid=(count,),
         in_specs=[
-            pl.BlockSpec((1, height, width), lambda i: (i, 0, 0)),
+            smem(),
+            *[pl.BlockSpec((1, share, width), lambda i: (i, 0, 0))] * len(pieces),
             pl.BlockSpec((3 * rank, height), lambda i: (0, i)),
             whole(u3.shape),
             pl.BlockSpec((rank, height), lambda i: (0, i)),
@@ -305,7 +320,7 @@
             8 * count * height * width * rank, 4 * count * height * width
         ),
         name="merge",
-    )(base, l3, u3, lower_t.astype(BF))
+    )(place, *pieces, l3, u3, lower_t.astype(BF))
 
 
 def qkv_body(tok_ref, gain_ref, w_ref, l_ref, ratio_ref, cos_ref, sin_ref,
@@ -597,9 +612,7 @@
     count, block, width = res_ref.shape
     step, me = pl.program_id(0), lax.axis_index("mp")
     row_sums = RowSum(me, scratch[:4], dot_ref)
-    half = (len(scratch) - 4) // 2
-    back_sums = Scatter(me, count, scratch[4:4 + half], back_out)
-    down_sums = Scatter(me, count, scratch[4 + half:], down_out)
+    back_sums = Scatter(me, count, scratch[4:], back_out)
 
     @pl.when(step == 0)
     def _():
@@ -608,7 +621,6 @@
             ref[...] = jnp.zeros_like(ref)
 
     back_sums.advance(step)
-    down_sums.advance(step)
     row_sums.advance(step)
 
     @pl.when(step < back_sums.blocks)
@@ -631,9 +643,6 @@
         sigmoid_g = jax.nn.sigmoid(gate_act)
         silu_g = gate_act * sigmoid_g
         hidden = (silu_g * lift_act).astype(BF)
-        for ref, place, at in down_sums.chunks(width):
-            ref[place] = dot_nn(hidden, down_ref[:, at]).astype(BF)
-        down_sums.copy(0, step, 0).start()
         grad_hidden = dot_nt(grad_down, down_ref[...])
         d_lift = grad_hidden * silu_g
         d_gate = grad_hidden * lift_act * sigmoid_g * (1.0 + gate_act * (1.0 - sigmoid_g))
@@ -644,6 +653,9 @@
                 dot_nt(grad_g, gate_ref[at, :]) + dot_nt(grad_l, lift_ref[at, :])
             ).astype(BF)
         back_sums.copy(0, step, 0).start()
+        for c in range(count):
+            cols = slice(c * width, (c + 1) * width)
+            down_out[c] = dot_nn(hidden, down_ref[:, cols]).astype(BF)
         product_g, product_l = inner_g * d_gate, inner_u * d_lift
         sg_ref[...] += jnp.sum(product_g, axis=0, keepdims=True)
         sl_ref[...] += jnp.sum(product_l, axis=0, keepdims=True)
@@ -681,19 +693,18 @@
             *[once(a.shape) for a in (gate, lift, down, rg, rl, lgl, ug, ul, ld, ud)],
         ],
         out_specs=[
-            whole((length, width)), whole((length, width)),
+            chunk_upto(blocks - 1, count, block, width), whole((length, width)),
             upto(blocks - 1, block, 1), whole((length, 1)),
             *[whole(s) for s in acc_shapes],
         ],
         out_shape=[
-            sds((length, width), BF), sds((length, width), BF),
+            sds((count, length, width), BF), sds((length, width), BF),
             sds((length, 1), F32), sds((length, 1), F32),
             *[sds(s, F32) for s in acc_shapes],
         ],
         scratch_shapes=[
             pltpu.VMEM((block, depth), BF), pltpu.VMEM((block, depth), BF),
             *row_scratch(count, blocks, block),
-            *scatter_scratch(count, blocks, block, width),
             *scatter_scratch(count, blocks, block, width),
         ],
         compiler_params=pltpu.CompilerParams(collective_id=2, has_side_effects=True),
@@ -1000,14 +1011,15 @@
 
 
 def gather_small(value, me):
-    part = value[None]
-    for bit in range(lax.axis_size("mp").bit_length() - 1):
+    levels = lax.axis_size("mp").bit_length() - 1
+    part = value.reshape((1,) * levels + value.shape)
+    for bit in range(levels - 1, -1, -1):
         came = flip(part, bit)
         upper = ((me >> bit) & 1) == 1
         part = jnp.concatenate(
-            [jnp.where(upper, came, part), jnp.where(upper, part, came)], axis=0
-        )
-    return part
+            [jnp.where(upper, came, part), jnp.where(upper, part, came)], axis=levels - 1 - bit
+        )
+    return part.reshape((1 << levels,) + value.shape)
 
 
 def scatter_cols(value, me):
@@ -1087,9 +1099,9 @@
     gain_a, gain_f = packed[5 * R], packed[5 * R + 1]
 
     output_w, square_o, cross_o = merge(
-        tie(output_base, qkv_arranged)[None], output_lower.T, output_upper)
+        [tie(output_base, qkv_arranged)[None]], output_lower.T, output_upper)
     down_w, square_d, cross_d = merge(
-        tie(down_base, qkv_arranged)[None], down_lower.T, down_upper)
+        [tie(down_base, qkv_arranged)[None]], down_lower.T, down_upper)
     row_stats = scatter_cols(
         jnp.concatenate([square_o, square_d, cross_o, cross_d], axis=0), me
     )
@@ -1104,17 +1116,30 @@
 
     upper_qkv = block_diagonal([own_cols(u, width) for u in (query_upper, key_upper, value_upper)])
     upper_g, upper_l = own_cols(gate_upper, hidden), own_cols(lift_upper, hidden)
-    qkv_w, square_qkv, cross_all = merge(qkv_base, lower_qkv_t, upper_qkv)
+    qkv_w, square_qkv, cross_all = merge([qkv_base], lower_qkv_t, upper_qkv)
     qkv_w = qkv_w.reshape(depth, 3 * width)
     norm_qkv = jnp.sqrt(square_qkv[0])
     scale_qkv = jnp.concatenate([query_scale, key_scale, value_scale])
     ratio_qkv = (scale_qkv / norm_qkv)[None]
     inv_ratio = 1.0 / ratio_qkv
 
-    gl_arranged = arrange([gate_base, lift_base], members)
-    gl_base = exchange(tie(gl_arranged, tok_all[0]))
+    copies, z = lax.axis_size("dp"), lax.axis_index("dp")
+    share = width // copies
+    gl_arranged = arrange(
+        [
+            lax.dynamic_slice_in_dim(tie(v, qkv_arranged), z * share, share, 0)
+            for v in (gate_base, lift_base)
+        ],
+        members,
+    )
+    gl_own = exchange(tie(gl_arranged, qkv_base))
+    from_low, from_high = [gl_own], [gl_own]
+    for _ in range(1, copies):
+        from_low.append(lax.ppermute(from_low[-1], "dp", [(i, i + 1) for i in range(copies - 1)]))
+        from_high.append(lax.ppermute(from_high[-1], "dp", [(i + 1, i) for i in range(copies - 1)]))
+    gl_pieces = from_low[:0:-1] + from_high
     gate_w, lift_w, square_gl, cross_g, cross_l = merge(
-        gl_base, lower_gl_t, block_diagonal([upper_g, upper_l]), [hidden, hidden]
+        gl_pieces, lower_gl_t, block_diagonal([upper_g, upper_l]), [hidden, hidden]
     )
     gate_w, lift_w = gate_w.reshape(depth, hidden), lift_w.reshape(depth, hidden)
     norm_gl = jnp.sqrt(square_gl[0])
@@ -1156,7 +1181,7 @@
             res = tie(st["residual_all"], state[s + 1]["residual_low"])
         else:
             res = tie(st["residual_all"], state[s - 1]["grad_output_low"])
-        st["inner_d"], back, st["inv_f"], dot_f, *st["ffn"] = ffn(
+        st["down"], back, st["inv_f"], dot_f, *st["ffn"] = ffn(
             res, chunk_gain_f, gd_all[s], gate_w, lift_w, down_w,
             ratio_g, ratio_l, low_l_gl, low_u_g, low_u_l, low_l_d, low_u_d,
         )
@@ -1168,9 +1193,6 @@
         st["grad_residual"] = grad_residual
         st["grad_output_low"] = (grad_residual * ratio_o).astype(BF)
         st["grad_output"] = gather(st["grad_output_low"])
-        inner_d = st["inner_d"].astype(F32)
-        st["out"] = (st["residual"] + inner_d * ratio_d).astype(BF)
-        st["g_d"] = jnp.sum(inner_d * grad_tops[s], axis=0)
         st["g_o"] = jnp.sum(st["inner_o"] * grad_residual, axis=0)
 
     def attention_back_stage(s):
@@ -1183,10 +1205,12 @@
         grad_att, st["a_o"], st["b_o"] = out_back(
             grad, st["att"], output_w, low_u_o, low_l_o
         )
+        st["grad_att"] = grad_att
         grads = attend_backward(
             st["lo"], st["start"], st["q"], st["k"], st["y"], grad_att, st["att"],
             st["lse"], st["cos"], st["sin"], ratio_qkv, block,
         )
+        st["grads"] = grads
         st["dx"], dot_a, st["a_qkv"], st["b_qkv"], st["g_qkv"] = qkv_backward(
             grads, st["y"], st["x"], st["xl"], qkv_w, low_u_qkv, inv_ratio, members
         )
@@ -1196,7 +1220,15 @@
             - tokens[s].astype(F32) * (inv * inv * dot_a / depth)
         )
 
-    for stage in (attention_stage, ffn_stage, attention_back_stage):
+    def late_stage(s):
+        st = state[s]
+        down = tie(st["down"], state[0]["grad_att"] if s == 0 else state[0]["grads"])
+        inner_d = lax.psum_scatter(down, "mp", scatter_dimension=0, tiled=False)
+        inner_d = inner_d.astype(F32)
+        st["out"] = (st["residual"] + inner_d * ratio_d).astype(BF)
+        st["g_d"] = jnp.sum(inner_d * grad_tops[s], axis=0)
+
+    for stage in (attention_stage, ffn_stage, attention_back_stage, late_stage):
         for s in range(seqs):
             stage(s)
 

time: 996 us -> 1030 us (1.034)
  blocking collectives: 0 us -> 33.5 us
  Pallas kernels: 727 us -> 696 us
  waiting for transfers between devices: 82.5 us -> 105 us
    ppermute x0 -> x6, waiting for transfers between devices: none -> 71.6 us  [the longest x3 70.4 us: on_device(): lax.ppermute(from_high[-1], 'dp', [(i + 1, i) for i in range(copies - 1)])]
    pallas_call x2, Pallas kernels: 258 us -> 200 us  [ffn(): pl.pallas_call(ffn_body, grid=(blocks + levels,), in_specs=[chunk_upto(bl...]
    all_to_all x2 -> x1, waiting for transfers between devices: 53.9 us -> 0.01 us  [exchange(): return lax.all_to_all(value, 'mp', split_axis=0, concat_axis=0, tiled=True)]
    pallas_call x2, Pallas kernels: 114 us -> 158 us  [qkv_backward(): pl.pallas_call(qkv_back_body, grid=(blocks + levels,), in_specs=[upto(blo...]
    all_to_all x0 -> x1, blocking collectives: none -> 33.5 us  [exchange(): return lax.all_to_all(value, 'mp', split_axis=0, concat_axis=0, tiled=True)]
    ppermute x0 -> x6, starting transfers between devices: none -> 20.9 us  [the longest x3 17 us: on_device(): lax.ppermute(from_low[-1], 'dp', [(i, i + 1) for i in range(copies - 1)])]
    all_gather x8, waiting for transfers between devices: 0.09 us -> 18.1 us  [gather(): return lax.all_gather(value, 'mp', axis=0)]
    pallas_call x2, Pallas kernels: 133 us -> 118 us  [out_forward(): pl.pallas_call(out_body, grid=(blocks + levels,), in_specs=[upto(blocks -...]
  transfers between devices with their start and end apart: 16 -> 23, of which waited for: 5 -> 10; matrix products, arithmetic and copies ran while one was open for 10% -> 11% of each run, Pallas kernels for 60% -> 64%
where the time goes in v1:
time: 1030 us; the launch traced here: 1020 us
  Pallas kernels  696 us (68%)
  waiting for transfers between devices  105 us (10%)
  other arithmetic  86 us (8%)
  local copies, waits for them, and re-layouts  49.5 us (5%)
  blocking collectives  33.5 us (3%)
  starting transfers between devices  33.1 us (3%)
  between operations  16 us (2%)
    pallas_call x2, Pallas kernels, ffn(): pl.pallas_call(ffn_body, grid=(blocks + levels,), in_specs=[chunk_upto(bl...  200 us
    pallas_call x2, Pallas kernels, qkv_backward(): pl.pallas_call(qkv_back_body, grid=(blocks + levels,), in_specs=[upto(blo...  158 us
    pallas_call x2, Pallas kernels, out_forward(): pl.pallas_call(out_body, grid=(blocks + levels,), in_specs=[upto(blocks -...  118 us
    ppermute x3, waiting for transfers between devices, on_device(): lax.ppermute(from_high[-1], 'dp', [(i + 1, i) for i in range(copies - 1)])  70.4 us
    pallas_call x2, Pallas kernels, attend_backward(): pl.pallas_call(functools.partial(attend_back_body, block=block), grid=(1,...  48.6 us
    pallas_call x1, Pallas kernels, reduce_sums(): pl.pallas_call(functools.partial(reduce_body, levels=levels, depths=depth...  43.3 us
    pallas_call x2, Pallas kernels, attend_forward(): pl.pallas_call(functools.partial(attend_body, block=block), grid=(1,), in...  41 us
    all_to_all x1, blocking collectives, exchange(): return lax.all_to_all(value, 'mp', split_axis=0, concat_axis=0, tiled=True)  33.5 us
  transfers between devices with their start and end apart: 23, of which 10 were waited for; matrix products, arithmetic and copies ran while one was open for 11% of the time, Pallas kernels for 64%

profile of v1, /device:TPU:0, one launch (start us, length us, event | category | flops | bytes accessed | tf_op | source)
XLA Modules:
  0.0 1019.3 jit_solution(3699284046040254876)
XLA Ops:
  7.2 3.0 fusion.55
  11.0 3.1 arrange.2
  14.2 5.3 all-to-all-start
  19.6 2.2 concatenate.107
  27.1 2.8 merge.5
  34.1 4.6 merge.6
  47.0 9.1 multiply_sine_fusion
  58.7 2.6 constant_dynamic-slice_fusion.10
  62.0 2.4 arrange.3
  70.6 3.3 collective-permute-done.4
  74.0 2.1 collective-permute-start.1
  76.1 2.9 collective-permute-done.5
  79.0 6.1 collective-permute-done.1
  91.4 7.6 merge.4
  100.9 16.0 %qkv_forward.2 = (bf16[2048,2048]{1,0:T(8,128)(2,1)}, bf16[2048,768]{1,0:T(8,128)(2,1)}, bf16[2048,256]{1,0:T(8,128)(2,1)}, bf16[2048,256]{1,0:T(8,128)(2,1)}, b...) custom-call(bf16[8,2048,256]{2,1,0:T(8,128)(2,1)} %all-gather.13.cloned.1.call-done.tok_ref, ...), custom_call_target="tpu_custom_call" | custom-call | flops 7516192768 | bytes 25165824 | tf_op jit(solution)/shard_map/qkv_forward/pallas_call | solution.py:354
  116.9 20.1 %attend_forward.2 = (bf16[2048,256]{1,0:T(8,128)(2,1)}, f32[2,8,256]{2,1,0:T(8,128)}) custom-call(s32[8]{0:T(128)} %and_select_fusion.1.lo_ref, s32[8,256]{1,0:T(8,128)} %copy-done.65, bf16[2048,256]{1,0:T(8,128)(2,1)} %get-tuple-element.128.q_ref, bf16[2048,256]{1,0:T(8,128)(2,1)} %get-tuple-element.129.k_ref, bf16[2048,768]{1,0:T(8,128)(2,1)} %get-tuple-element.130.v_ref.y_ref), custom_call_target="tpu_custom_call" | custom-call | flops 2147483648 | bytes 4194304 | tf_op jit(solution)/shard_map/attend_forward/pallas_call | solution.py:442
  137.0 63.5 %out_forward.2 = bf16[2048,256]{1,0:T(8,128)(2,1)} custom-call(bf16[2048,256]{1,0:T(8,128)(2,1)} %get-tuple-element.131.a_ref.o_ref, bf16[256,2048]{1,0:T(8,128)(2,1)} %bitcast.243), custom_call_target="tpu_custom_call" | custom-call | flops 2147483648 | bytes 167772160 | tf_op jit(solution)/shard_map/out_forward/pallas_call | solution.py:594
  200.6 2.5 fusion.22
  203.9 2.9 fusion.11
  207.2 33.5 %all_to_all.10.refs_3_ = bf16[8,64,1408]{2,1,0:T(8,128)(2,1)S(1)} all-to-all(bf16[8,64,1408]{2,1,0:T(8,128)(2,1)} %arrange.3), channel_id=1, replica_groups=mesh['dp'=4,'mp'=8] {'mp'}, dimensions={0} | all-to-all | bytes 2883584 | tf_op jit(solution)/shard_map/all_to_all | solution.py:1083
  242.0 5.7 collective-permute-start.6
  247.7 28.1 %collective-permute-done.9.refs_4_ = bf16[8,64,1408]{2,1,0:T(8,128)(2,1)} collective-permute-done((bf16[8,64,1408]{2,1,0:T(8,128)(2,1)S(1)}, bf16[8,64,1408]{2,1,0:T(8,128)(2,1)}, u32[]{:S(2)}, u32[]{:S(2)}) %collective-permute-start.9) | collective-permute-done | bytes 1441824 | tf_op jit(solution)/shard_map/ppermute | solution.py:1139
  277.1 5.7 collective-permute-start.7
  287.4 22.9 %collective-permute-done.10.refs_5_ = bf16[8,64,1408]{2,1,0:T(8,128)(2,1)} collective-permute-done((bf16[8,64,1408]{2,1,0:T(8,128)(2,1)}, bf16[8,64,1408]{2,1,0:T(8,128)(2,1)}, u32[]{:S(2)}, u32[]{:S(2)}) %collective-permute-start.10) | collective-permute-done | bytes 1441824 | tf_op jit(solution)/shard_map/ppermute | solution.py:1139
  311.6 5.7 collective-permute-start.8
  317.8 2.9 pad_maximum_fusion.4.cos_ref
  324.6 19.3 %collective-permute-done.11.refs_6_ = bf16[8,64,1408]{2,1,0:T(8,128)(2,1)} collective-permute-done((bf16[8,64,1408]{2,1,0:T(8,128)(2,1)}, bf16[8,64,1408]{2,1,0:T(8,128)(2,1)}, u32[]{:S(2)}, u32[]{:S(2)}) %collective-permute-start.11) | collective-permute-done | bytes 1441824 | tf_op jit(solution)/shard_map/ppermute | solution.py:1139
  345.1 10.7 %merge.7 = (bf16[8,256,704]{2,1,0:T(8,128)(2,1)}, bf16[8,256,704]{2,1,0:T(8,128)(2,1)}, f32[1,1408]{1,0:T(1,128)}, f32[32,704]{1,0:T(8,128)}, f32[32,704]{1,0:T(8,128)}) custom-call(s32[1]{0:T(128)} %bitcast.15.place_ref, bf16[8,64,1408]{2,1,0:T(8,128)(2,1)} %collective-permute-done.8.refs_0_, bf16[8,64,1408]{2,1,0:T(8,128)(2,1)} %collective-permute-done.7.refs_1_, ...), custom_call_target="tpu_custom_call" | custom-call | flops 738197504 | bytes 11534336 | tf_op jit(solution)/shard_map/merge/pallas_call | solution.py:299
  355.9 15.9 %qkv_forward.3 = (bf16[2048,2048]{1,0:T(8,128)(2,1)}, bf16[2048,768]{1,0:T(8,128)(2,1)}, bf16[2048,256]{1,0:T(8,128)(2,1)}, bf16[2048,256]{1,0:T(8,128)(2,1)}, b...) custom-call(bf16[8,2048,256]{2,1,0:T(8,128)(2,1)} %all-gather.15.cloned.1.call-done.tok_ref, ...), custom_call_target="tpu_custom_call" | custom-call | flops 7516192768 | bytes 25165824 | tf_op jit(solution)/shard_map/qkv_forward/pallas_call | solution.py:354
  371.8 20.8 %attend_forward.3 = (bf16[2048,256]{1,0:T(8,128)(2,1)}, f32[2,8,256]{2,1,0:T(8,128)}) custom-call(s32[8]{0:T(128)} %and_select_fusion.lo_ref, s32[8,256]{1,0:T(8,128)} %reshape.266.start_ref, bf16[2048,256]{1,0:T(8,128)(2,1)} %get-tuple-element.140.q_ref, bf16[2048,256]{1,0:T(8,128)(2,1)} %get-tuple-element.141.k_ref, ...), custom_call_target="tpu_custom_call" | custom-call | flops 2147483648 | bytes 4194304 | tf_op jit(solution)/shard_map/attend_forward/pallas_call | solution.py:442
  392.7 54.4 %out_forward.3 = bf16[2048,256]{1,0:T(8,128)(2,1)} custom-call(bf16[2048,256]{1,0:T(8,128)(2,1)} %get-tuple-element.147.a_ref.o_ref, bf16[256,2048]{1,0:T(8,128)(2,1)} %bitcast.244), custom_call_target="tpu_custom_call" | custom-call | flops 2147483648 | bytes 167772160 | tf_op jit(solution)/shard_map/out_forward/pallas_call | solution.py:594
  447.1 2.6 fusion.23
  455.6 102.2 %ffn.2 = (bf16[8,2048,256]{2,1,0:T(8,128)(2,1)}, bf16[2048,256]{1,0:T(8,128)(2,1)}, f32[2048,1]{1,0:T(8,128)}, f32[2048,1]{1,0:T(8,128)}, f32[128,2048]{1,0:T(8,...) custom-call(bf16[8,2048,256]{2,1,0:T(8,128)(2,1)} %bitcast.229, ...), custom_call_target="tpu_custom_call" | custom-call | flops 41339060224 | bytes 167772160 | tf_op jit(solution)/shard_map/ffn/pallas_call | solution.py:686
  557.9 2.9 fusion.50
  561.1 2.9 fusion
  566.8 18.0 %all-gather.19.cloned.1.call-done.gd_in_ref = bf16[8,2048,256]{2,1,0:T(8,128)(2,1)} async-done(((bf16[1,2048,256]{2,1,0:T(8,128)(2,1)}), bf16[8,2048,256]{2,1,0:T(8,128)(2,1)}) %all-gather.19.cloned.1.call-update) | async-done | bytes 8388624 | tf_op jit(solution)/shard_map/all_gather | solution.py:1077
  584.8 97.8 %ffn.3 = (bf16[8,2048,256]{2,1,0:T(8,128)(2,1)}, bf16[2048,256]{1,0:T(8,128)(2,1)}, f32[2048,1]{1,0:T(8,128)}, f32[2048,1]{1,0:T(8,128)}, f32[128,2048]{1,0:T(8,...) custom-call(bf16[8,2048,256]{2,1,0:T(8,128)(2,1)} %bitcast.231, ...), custom_call_target="tpu_custom_call" | custom-call | flops 41339060224 | bytes 167772160 | tf_op jit(solution)/shard_map/ffn/pallas_call | solution.py:686
  682.7 2.3 fusion.49
  685.0 3.1 fusion.1
  692.4 12.4 %out_back.2 = (bf16[2048,256]{1,0:T(8,128)(2,1)}, f32[128,256]{1,0:T(8,128)}, f32[128,2048]{1,0:T(8,128)}) custom-call(bf16[8,2048,256]{2,1,0:T(8,128)(2,1)} %bitcast.232, bf16[2048,256]{1,0:T(8,128)(2,1)} %get-tuple-element.131.a_ref.o_ref, bf16[256,2048]{1,0:T(8,128)(2,1)} %bitcast.245, bf16[128,2048]{1,0:T(8,128)(2,1)} %pad.101.u_ref, ...), custom_call_target="tpu_custom_call" | custom-call | flops 4294967296 | bytes 12582912 | tf_op jit(solution)/shard_map/out_back/pallas_call | solution.py:737
  704.8 23.9 %attend_backward.2.g_ref = bf16[2048,768]{1,0:T(8,128)(2,1)} custom-call(s32[8]{0:T(128)} %and_select_fusion.1.lo_ref, s32[8,256]{1,0:T(8,128)} %copy-done.65, bf16[2048,256]{1,0:T(8,128)(2,1)} %get-tuple-element.128.q_ref, bf16[2048,256]{1,0:T(8,128)(2,1)} %get-tuple-element.129.k_ref, bf16[2048,768]{1,0:T(8,128)(2,1)} %get-tuple-element.130.v_ref.y_ref, ...), custom_call_target="tpu_custom_call" | custom-call | flops 5368709120 | bytes 8388608 | tf_op jit(solution)/shard_map/attend_backward/pallas_call | solution.py:541
  743.2 73.5 %qkv_backward.2 = (bf16[2048,256]{1,0:T(8,128)(2,1)}, f32[2048,1]{1,0:T(8,128)}, f32[128,2048]{1,0:T(8,128)}, f32[128,768]{1,0:T(8,128)}, f32[1,768]{1,0:T(1,128)}) custom-call(bf16[2048,768]{1,0:T(8,128)(2,1)} %attend_backward.2.g_ref, bf16[2048,768]{1,0:T(8,128)(2,1)} %get-tuple-element.130.v_ref.y_ref, bf16[2048,2048]{1,0:T(8,128)(2,1)} %get-tuple-element.166.x_ref, ...), custom_call_target="tpu_custom_call" | custom-call | flops 12884901888 | bytes 167772160 | tf_op jit(solution)/shard_map/qkv_backward/pallas_call | solution.py:789
  816.7 12.3 %out_back.3 = (bf16[2048,256]{1,0:T(8,128)(2,1)}, f32[128,256]{1,0:T(8,128)}, f32[128,2048]{1,0:T(8,128)}) custom-call(bf16[8,2048,256]{2,1,0:T(8,128)(2,1)} %bitcast.230, bf16[2048,256]{1,0:T(8,128)(2,1)} %get-tuple-element.147.a_ref.o_ref, bf16[256,2048]{1,0:T(8,128)(2,1)} %bitcast.246, bf16[128,2048]{1,0:T(8,128)(2,1)} %pad.101.u_ref, ...), custom_call_target="tpu_custom_call" | custom-call | flops 4294967296 | bytes 12582912 | tf_op jit(solution)/shard_map/out_back/pallas_call | solution.py:737
  829.1 24.7 %attend_backward.3.g_ref = bf16[2048,768]{1,0:T(8,128)(2,1)} custom-call(s32[8]{0:T(128)} %and_select_fusion.lo_ref, s32[8,256]{1,0:T(8,128)} %reshape.266.start_ref, bf16[2048,256]{1,0:T(8,128)(2,1)} %get-tuple-element.140.q_ref, bf16[2048,256]{1,0:T(8,128)(2,1)} %get-tuple-element.141.k_ref, bf16[2048,768]{1,0:T(8,128)(2,1)} %get-tuple-element.142.v_ref.y_ref, ...), custom_call_target="tpu_custom_call" | custom-call | flops 5368709120 | bytes 8388608 | tf_op jit(solution)/shard_map/attend_backward/pallas_call | solution.py:541
  853.7 84.3 %qkv_backward.3 = (bf16[2048,256]{1,0:T(8,128)(2,1)}, f32[2048,1]{1,0:T(8,128)}, f32[128,2048]{1,0:T(8,128)}, f32[128,768]{1,0:T(8,128)}, f32[1,768]{1,0:T(1,128)}) custom-call(bf16[2048,768]{1,0:T(8,128)(2,1)} %attend_backward.3.g_ref, bf16[2048,768]{1,0:T(8,128)(2,1)} %get-tuple-element.142.v_ref.y_ref, bf16[2048,2048]{1,0:T(8,128)(2,1)} %get-tuple-element.174.x_ref, ...), custom_call_target="tpu_custom_call" | custom-call | flops 12884901888 | bytes 167772160 | tf_op jit(solution)/shard_map/qkv_backward/pallas_call | solution.py:789
  947.7 2.3 pad_maximum_fusion
  950.0 4.5 fusion.25
  955.2 43.3 %reduce_sums.1 = (f32[8,256]{1,0:T(8,128)}, f32[8,704]{1,0:T(8,128)}, f32[16,2048]{1,0:T(8,128)}, f32[16,2048]{1,0:T(8,128)}, f32[16,2048]{1,0:T(8,128)}, /*inde...) custom-call(f32[8,112,256]{2,1,0:T(8,128)} %bitcast.183, ...), custom_call_target="tpu_custom_call" | custom-call | bytes 60000000 | tf_op jit(solution)/shard_map/reduce_sums/pallas_call | solution.py:957
  (392 shorter events, 102.5 us)
Async XLA Ops:
  7.2 93.7 %all-gather.13.cloned.1.call-start = ((), (), s32[]{:S(2)}) async-start(), calls=%async_computation.4 | async-start | bytes 9437184 | tf_op jit(solution)/shard_map/all_gather | solution.py:1077
  10.3 345.6 %all-gather.15.cloned.1.call-start = ((), (), s32[]{:S(2)}) async-start(), calls=%async_computation.5 | async-start | bytes 9437184 | tf_op jit(solution)/shard_map/all_gather | solution.py:1077
  14.2 10.3 %copy-start.31 = (f32[256,16]{0,1:T(8,128)S(1)}, f32[256,16]{0,1:T(8,128)}, u32[]{:S(2)}) copy-start(f32[256,16]{0,1:T(8,128)} %param.51) | copy-start | bytes 49156
  14.2 11.5 %copy-start.24 = (f32[16,2048]{1,0:T(8,128)S(1)}, f32[16,2048]{1,0:T(8,128)}, u32[]{:S(2)}) copy-start(f32[16,2048]{1,0:T(8,128)} %refs_18_.1) | copy-start | bytes 393220
  14.2 75.5 %all-to-all-start = ((bf16[8,256,768]{2,1,0:T(8,128)(2,1)}), bf16[8,256,768]{2,1,0:T(8,128)(2,1)S(1)}, u32[]{:S(2)}, u32[]{:S(2)}) async-start(bf16[8,256,768]{2,1,0:T(8,128)(2,1)} %arrange.2), calls=%async_computation | async-start | bytes 6291456 | tf_op jit(solution)/shard_map/all_to_all | solution.py:1083
  19.6 13.2 %copy-start.25 = (f32[16,2048]{1,0:T(8,128)S(1)}, f32[16,2048]{1,0:T(8,128)}, u32[]{:S(2)}) copy-start(f32[16,2048]{1,0:T(8,128)} %refs_21_.1) | copy-start | bytes 393220
  19.6 436.0 %all-gather.21.cloned.1.call-start = ((), (), s32[]{:S(2)}) async-start(), calls=%async_computation.10 | async-start | bytes 9437184 | tf_op jit(solution)/shard_map/all_gather | solution.py:1077
  22.5 47.2 %collective-permute-start = (f32[1,1,1,88,256]{4,3,2,1,0:T(8,128)}, f32[1,1,1,88,256]{4,3,2,1,0:T(8,128)}, u32[]{:S(2)}, u32[]{:S(2)}) collective-permute-start(f32[1,1,1,88,256]{4,3,2,1,0:T(8,128)} %pad_bitcast_fusion.1), channel_id=1, source_target_pairs={{0,4},{1,5},{2,6},{3,7},{4,0},{5,1},{6,2},{7,3},{8,12},{9,13},{10,... | collective-permute-start | bytes 270344 | tf_op jit(solution)/shard_map/ppermute | solution.py:1010
  29.9 8.8 copy-start.78
  43.2 22.8 %collective-permute-start.3 = (f32[4,34,256]{2,0,1:T(4,128)}, f32[4,34,256]{2,0,1:T(4,128)}, u32[]{:S(2)}, u32[]{:S(2)}) collective-permute-start(f32[4,34,256]{2,0,1:T(4,128)} %bitcast.178), channel_id=1, source_target_pairs={{0,1},{1,0},{2,3},{3,2},{4,5},{5,4},{6,7},{7,6},{8,9},{9,8},{10,11... | collective-permute-start | bytes 417800 | tf_op jit(solution)/shard_map/ppermute | solution.py:1010
  44.3 11.8 %copy-start.54 = (s32[2048]{0:T(1024)}, s32[2048]{0:T(1024)S(1)}, u32[]{:S(2)}) copy-start(s32[2048]{0:T(1024)S(1)} %get-tuple-element.238) | copy-start | bytes 24580
  46.4 15.0 %copy-start.32 = (f32[16,256]{1,0:T(8,128)}, f32[16,256]{1,0:T(8,128)S(1)}, u32[]{:S(2)}) copy-start(f32[16,256]{1,0:T(8,128)S(1)} %get-tuple-element.332) | copy-start | bytes 49156
  46.4 15.0 %copy-start.34 = (f32[16,256]{1,0:T(8,128)}, f32[16,256]{1,0:T(8,128)S(1)}, u32[]{:S(2)}) copy-start(f32[16,256]{1,0:T(8,128)S(1)} %get-tuple-element.333) | copy-start | bytes 49156
  64.4 21.4 %copy-start.94 = (f32[256]{0:T(256)S(1)}, f32[256]{0:T(256)}, u32[]{:S(2)}) copy-start(f32[256]{0:T(256)} %param.53) | copy-start | bytes 3076
  67.2 6.7 collective-permute-start.4
  73.9 5.1 collective-permute-start.5
  74.0 11.0 %collective-permute-start.1 = (f32[2,1,1,88,256]{4,3,2,1,0:T(8,128)S(1)}, f32[2,1,1,88,256]{4,3,2,1,0:T(8,128)S(1)}, u32[]{:S(2)}, u32[]{:S(2)}) collective-permute-start(f32[2,1,1,88,256]{4,3,2,1,0:T(8,128)S(1)} %pad_maximum_fusion.16), channel_id=1, source_target_pairs={{0,2},{1,3},{2,0},{3,1},{4,6},{5,7},{6,4},{7,5},{8,10},{9,11},{10,... | collective-permute-start | bytes 540680 | tf_op jit(solution)/shard_map/ppermute | solution.py:1010
  79.0 8.0 copy-start.36
  85.1 1.7 collective-permute-start.2
  86.4 114.2 %copy-start.55 = (f32[256]{0:T(256)}, f32[256]{0:T(256)S(1)}, u32[]{:S(2)}) copy-start(f32[256]{0:T(256)S(1)} %get-tuple-element.318) | copy-start | bytes 3076
  89.7 9.3 copy-start.86
  89.7 9.3 copy-start.88
  89.7 9.3 copy-start.90
  137.0 63.5 %copy-start = (bf16[2,2048,256]{2,1,0:T(8,128)(2,1)S(1)}, bf16[2,2048,256]{2,1,0:T(8,128)(2,1)}, u32[]{:S(2)}) copy-start(bf16[2,2048,256]{2,1,0:T(8,128)(2,1)} %param.33) | copy-start | bytes 6291460
  203.2 252.4 %all-gather.17.cloned.1.call-start = ((), (), s32[]{:S(2)}) async-start(), calls=%async_computation.6 | async-start | bytes 9437184 | tf_op jit(solution)/shard_map/all_gather | solution.py:1077
  206.8 360.0 %all-gather.25.cloned.1.call-start = ((), (), s32[]{:S(2)}) async-start(), calls=%async_computation.12 | async-start | bytes 9437184 | tf_op jit(solution)/shard_map/all_gather | solution.py:1077
  240.7 81.4 %copy-start.9 = (bf16[8,64,1408]{2,1,0:T(8,128)(2,1)}, bf16[8,64,1408]{2,1,0:T(8,128)(2,1)S(1)}, u32[]{:S(2)}) copy-start(bf16[8,64,1408]{2,1,0:T(8,128)(2,1)S(1)} %all_to_all.10.refs_3_) | copy-start | bytes 4325380
  240.7 35.1 %collective-permute-start.9 = (bf16[8,64,1408]{2,1,0:T(8,128)(2,1)S(1)}, bf16[8,64,1408]{2,1,0:T(8,128)(2,1)}, u32[]{:S(2)}, u32[]{:S(2)}) collective-permute-start(bf16[8,64,1408]{2,1,0:T(8,128)(2,1)S(1)} %all_to_all.10.refs_3_), channel_id=1, source_target_pairs={{8,0},{16,8},{24,16},{9,1},{17,9},{25,17},{10,2},{18,10},{26,18},{... | collective-permute-start | bytes 4325384 | tf_op jit(solution)/shard_map/ppermute | solution.py:1139
  242.0 35.1 %collective-permute-start.6 = (bf16[8,64,1408]{2,1,0:T(8,128)(2,1)S(1)}, bf16[8,64,1408]{2,1,0:T(8,128)(2,1)}, u32[]{:S(2)}, u32[]{:S(2)}) collective-permute-start(bf16[8,64,1408]{2,1,0:T(8,128)(2,1)S(1)} %all_to_all.10.refs_3_), channel_id=1, source_target_pairs={{0,8},{8,16},{16,24},{1,9},{9,17},{17,25},{2,10},{10,18},{18,26},{... | collective-permute-start | bytes 4325384 | tf_op jit(solution)/shard_map/ppermute | solution.py:1138
  275.8 34.5 %collective-permute-start.10 = (bf16[8,64,1408]{2,1,0:T(8,128)(2,1)}, bf16[8,64,1408]{2,1,0:T(8,128)(2,1)}, u32[]{:S(2)}, u32[]{:S(2)}) collective-permute-start(bf16[8,64,1408]{2,1,0:T(8,128)(2,1)} %collective-permute-done.9.refs_4_), channel_id=1, source_target_pairs={{8,0},{16,8},{24,16},{9,1},{17,9},{25,17},{10,2},{18,10},{26,18},{... | collective-permute-start | bytes 4325384 | tf_op jit(solution)/shard_map/ppermute | solution.py:1139
  277.1 34.5 %collective-permute-start.7 = (bf16[8,64,1408]{2,1,0:T(8,128)(2,1)}, bf16[8,64,1408]{2,1,0:T(8,128)(2,1)}, u32[]{:S(2)}, u32[]{:S(2)}) collective-permute-start(bf16[8,64,1408]{2,1,0:T(8,128)(2,1)} %collective-permute-done.6.refs_2_), channel_id=1, source_target_pairs={{0,8},{8,16},{16,24},{1,9},{9,17},{17,25},{2,10},{10,18},{18,26},{... | collective-permute-start | bytes 4325384 | tf_op jit(solution)/shard_map/ppermute | solution.py:1138
  284.1 36.6 %copy-start.10 = (f32[2048,64]{1,0:T(8,128)S(1)}, f32[2048,64]{1,0:T(8,128)}, u32[]{:S(2)}) copy-start(f32[2048,64]{1,0:T(8,128)} %get-tuple-element.298) | copy-start | bytes 1572868
  284.1 36.6 %copy-start.11 = (f32[2048,64]{1,0:T(8,128)S(1)}, f32[2048,64]{1,0:T(8,128)}, u32[]{:S(2)}) copy-start(f32[2048,64]{1,0:T(8,128)} %get-tuple-element.299) | copy-start | bytes 1572868
  310.3 33.6 %collective-permute-start.11 = (bf16[8,64,1408]{2,1,0:T(8,128)(2,1)}, bf16[8,64,1408]{2,1,0:T(8,128)(2,1)}, u32[]{:S(2)}, u32[]{:S(2)}) collective-permute-start(bf16[8,64,1408]{2,1,0:T(8,128)(2,1)} %collective-permute-done.10.refs_5_), channel_id=1, source_target_pairs={{8,0},{16,8},{24,16},{9,1},{17,9},{25,17},{10,2},{18,10},{26,18},{... | collective-permute-start | bytes 4325384 | tf_op jit(solution)/shard_map/ppermute | solution.py:1139
  311.6 33.5 %collective-permute-start.8 = (bf16[8,64,1408]{2,1,0:T(8,128)(2,1)}, bf16[8,64,1408]{2,1,0:T(8,128)(2,1)}, u32[]{:S(2)}, u32[]{:S(2)}) collective-permute-start(bf16[8,64,1408]{2,1,0:T(8,128)(2,1)} %collective-permute-done.7.refs_1_), channel_id=1, source_target_pairs={{0,8},{8,16},{16,24},{1,9},{9,17},{17,25},{2,10},{10,18},{18,26},{... | collective-permute-start | bytes 4325384 | tf_op jit(solution)/shard_map/ppermute | solution.py:1138
  392.7 54.4 %copy-start.56 = (f32[256]{0:T(256)S(1)}, f32[256]{0:T(256)}, u32[]{:S(2)}) copy-start(f32[256]{0:T(256)} %copy-done.55) | copy-start | bytes 3076
  449.7 135.1 %all-gather.19.cloned.1.call-start = ((), (), s32[]{:S(2)}) async-start(), calls=%async_computation.7 | async-start | bytes 9437184 | tf_op jit(solution)/shard_map/all_gather | solution.py:1077
  450.3 242.2 %all-gather.23.cloned.1.call-start = ((), (), s32[]{:S(2)}) async-start(), calls=%async_computation.11 | async-start | bytes 9437184 | tf_op jit(solution)/shard_map/all_gather | solution.py:1077
  455.6 105.2 %copy-start.8 = (bf16[2048,256]{1,0:T(8,128)(2,1)S(1)}, bf16[2048,256]{1,0:T(8,128)(2,1)}, u32[]{:S(2)}) copy-start(bf16[2048,256]{1,0:T(8,128)(2,1)} %out_forward.2) | copy-start | bytes 3145732
  566.6 250.1 %all-gather.27.cloned.1.call-start = ((), (), s32[]{:S(2)}) async-start(), calls=%async_computation.13 | async-start | bytes 9437184 | tf_op jit(solution)/shard_map/all_gather | solution.py:1077
  690.8 259.2 %reduce-scatter.5.cloned.1.call-start = ((), (), s32[]{:S(2)}) async-start(), calls=%async_computation.9 | async-start | bytes 9437184 | tf_op jit(solution)/shard_map/reduce_scatter | solution.py:1226
  728.7 221.2 %reduce-scatter.3.cloned.1.call-start = ((), (), s32[]{:S(2)}) async-start(), calls=%async_computation.8 | async-start | bytes 9437184 | tf_op jit(solution)/shard_map/reduce_scatter | solution.py:1226
  853.7 84.4 %copy-start.93 = (f32[1,768]{1,0:T(1,128)S(1)}, f32[1,768]{1,0:T(1,128)}, u32[]{:S(2)}) copy-start(f32[1,768]{1,0:T(1,128)} %get-tuple-element.190) | copy-start | bytes 9220
  955.2 46.2 %copy-start.12 = (bf16[1,2048,256]{2,1,0:T(8,128)(2,1)S(1)}, bf16[1,2048,256]{2,1,0:T(8,128)(2,1)}, u32[]{:S(2)}) copy-start(bf16[1,2048,256]{2,1,0:T(8,128)(2,1)} %get-tuple-element.251) | copy-start | bytes 3145732
  955.2 46.2 %copy-start.13 = (bf16[1,2048,256]{2,1,0:T(8,128)(2,1)S(1)}, bf16[1,2048,256]{2,1,0:T(8,128)(2,1)}, u32[]{:S(2)}) copy-start(bf16[1,2048,256]{2,1,0:T(8,128)(2,1)} %get-tuple-element.252) | copy-start | bytes 3145732
  1001.5 7.9 copy-start.68
  1001.5 8.5 copy-start.26
  1003.0 8.4 copy-start.45
  (71 other events, 236.8 us)
Sparse Core Ops, SparseCore 0:
  10.4 89.4 all-gather.12
  101.8 60.9 all-gather.14
  203.3 68.0 all-gather.20
  273.2 54.2 all-gather.16
  449.8 71.2 all-gather.24
  522.9 61.9 all-gather.18
  586.7 74.0 all-gather.22
  690.9 54.0 all-gather.26
  748.4 84.6 reduce-scatter.4
  836.5 97.6 reduce-scatter.2
